TPU v7x, 256 devices: a whole 4x4x8 slice. The times are simulated.
256 devices in a mesh: samples: 4 (over x), features: 32 (over z, y), rhs: 2 (over core).
Axes of the slice: x: 4, y: 4, z: 8, core: 2. Of those that a mesh axis runs over, the one named last changes fastest.
Arguments:
- design: bfloat16 [32768, 32768], P(('samples', 'rhs'), 'features'), may hold values from -0.03125 to 0.03125
- right_side: float32 [32768, 64], P('features', 'rhs'), may hold values from -6 to 6
- factor: bfloat16 [32768, 768], P('features', 'rhs'), may hold values from -0.03125 to 0.03125
- nystrom_values: float32 [768], replicated, may hold values from 0.5 to 3
Outputs:
- solution: float32 [32768, 64], P('features', 'rhs')
- residual: float32 [32768, 64], P('features', 'rhs')
All inputs are finite; a program needn't handle non-finite values.
Results may differ from a plain program's by a relative error of at most 0.0181.
Values may be sent and summed in bfloat16 or wider, within the bound.
A program may use at most 64 MiB of HBM per device.

v0:
```python
import jax
import jax.numpy as jnp
from jax import lax
from jax.sharding import PartitionSpec as P

ITERS = 3


ridge_weight = 1.0


def sent_to_all(array, axis):
    size = lax.axis_size(axis)
    return lax.all_to_all(
        jnp.broadcast_to(array[None], (size, *array.shape)), axis, 0, 0, tiled=True
    )


def joined_along(parts, dim):
    shape = list(parts.shape[1:])
    shape[dim] *= parts.shape[0]
    return jnp.moveaxis(parts, 0, dim).reshape(shape)


def gathered_copies(array, axis, dim):
    parts = sent_to_all(array, axis)
    return joined_along(parts, dim)


def padded_to(lines, size):
    spare = -lines.shape[0] % size
    if not spare:
        return lines
    return jnp.concatenate([lines, jnp.zeros((spare, *lines.shape[1:]), lines.dtype)])


def cut_along(array, dim, size):
    before, after = (array.shape[:dim], array.shape[dim + 1 :])
    return jnp.moveaxis(array.reshape(*before, size, -1, *after), dim, 0)


def summed_on_arrival(array, axis, dim):
    parts = cut_along(array, dim, lax.axis_size(axis))
    arrived = lax.all_to_all(parts, axis, split_axis=0, concat_axis=0, tiled=True)
    return arrived.sum(axis=0)


def total_of(array, axes):
    lines = array.reshape(-1, array.shape[-1])
    padded = padded_to(lines, lax.axis_size(axes))
    whole = gathered_copies(summed_on_arrival(padded, axes, 0), axes, 0)
    return lax.slice_in_dim(whole, 0, len(lines)).reshape(array.shape)


def taken_together(array, axis):
    return sent_to_all(array, axis).sum(axis=0)


def inner_prod(left, right):
    return lax.dot_general(
        left,
        right,
        (((0,), (0,)), ((), ())),
        precision=lax.Precision.HIGHEST,
        preferred_element_type=jnp.float32,
    )


def split_parts(values):
    upper = values.astype(jnp.bfloat16)
    widened = lax.optimization_barrier(upper).astype(jnp.float32)
    lower = (values - widened).astype(jnp.bfloat16)
    return (upper, lower)


def factor_inner(factor_narrow, values):
    upper, lower = split_parts(values)
    dims = (((0,), (0,)), ((), ()))
    first = lax.dot_general(factor_narrow, upper, dims, preferred_element_type=jnp.float32)
    second = lax.dot_general(factor_narrow, lower, dims, preferred_element_type=jnp.float32)
    return first + second


def factor_times(factor_narrow, values):
    upper, lower = split_parts(values)
    first = jnp.dot(factor_narrow, upper, preferred_element_type=jnp.float32)
    second = jnp.dot(factor_narrow, lower, preferred_element_type=jnp.float32)
    return first + second


def shards(design, right_side, factor, nystrom_values):
    feat_rows, col_share = right_side.shape
    shrink = (1.0 + jnp.min(nystrom_values)) / (1.0 + nystrom_values) - 1.0
    columns = gathered_copies(right_side, "rhs", 1)
    residual = columns
    basis_rows = gathered_copies(factor, "rhs", 1)

    def totals(values):
        return jax.tree.map(lambda part: total_of(part, "features"), values)

    def expand(projected):
        return factor_times(basis_rows, shrink[:, None] * projected)

    projected = totals(factor_inner(basis_rows, residual))
    direction = residual + expand(projected)
    solution = jnp.zeros_like(residual)
    for iteration in range(ITERS):
        narrow = direction.astype(jnp.bfloat16)
        apply_partial_value = jnp.dot(design, narrow, preferred_element_type=jnp.float32)
        narrow_images = total_of(apply_partial_value, "features").astype(jnp.bfloat16)
        feature_term = lax.dot_general(
            design, narrow_images, (((0,), (0,)), ((), ())), preferred_element_type=jnp.float32
        )
        summed = taken_together(feature_term, ("samples", "rhs"))
        applied = summed + ridge_weight * direction
        gram_block, cross_term, image_res, image_image, factor_image = totals(
            (
                inner_prod(direction, applied),
                inner_prod(direction, residual),
                inner_prod(applied, residual),
                inner_prod(applied, applied),
                factor_inner(basis_rows, applied),
            )
        )
        gram_block = 0.5 * (gram_block + gram_block.T)
        chol_lower = jnp.linalg.cholesky(gram_block)
        unit_dir = jax.scipy.linalg.solve_triangular(chol_lower, direction.T, lower=True).T
        unit_img = jax.scipy.linalg.solve_triangular(chol_lower, applied.T, lower=True).T
        step_coef = jax.scipy.linalg.solve_triangular(chol_lower, cross_term, lower=True)
        solution = solution + jnp.dot(unit_dir, step_coef, precision=lax.Precision.HIGHEST)
        residual = residual - jnp.dot(unit_img, step_coef, precision=lax.Precision.HIGHEST)
        if iteration + 1 < ITERS:
            back_step = jax.scipy.linalg.solve_triangular(
                chol_lower, step_coef, lower=True, trans=1
            )
            projected = projected - jnp.dot(
                factor_image, back_step, precision=lax.Precision.HIGHEST
            )
            scaled = residual + expand(projected)
            image_new = image_res - jnp.dot(image_image, back_step, precision=lax.Precision.HIGHEST)
            image_new = image_new + inner_prod(factor_image, shrink[:, None] * projected)
            next_coef = -jax.scipy.linalg.solve_triangular(chol_lower, image_new, lower=True)
            direction = scaled + jnp.dot(unit_dir, next_coef, precision=lax.Precision.HIGHEST)
    column_start = lax.axis_index("rhs") * col_share
    out_sol = lax.dynamic_slice_in_dim(solution, column_start, col_share, 1)
    out_res = lax.dynamic_slice_in_dim(residual, column_start, col_share, 1)
    return (out_sol, out_res)


def solution(mesh):
    placed = (P(("samples", "rhs"), "features"), P("features", "rhs"), P("features", "rhs"), P())
    return jax.shard_map(
        shards,
        mesh=mesh,
        in_specs=placed,
        out_specs=(P("features", "rhs"), P("features", "rhs")),
        check_vma=False,
    )
```

profile of v0, /device:TPU:1, one launch (start us, length us, event | category | flops | bytes accessed | tf_op | source)
XLA Modules:
  0.0 706.5 jit_solution(17275730974886748745)
XLA Ops:
  2.2 6.6 all-to-all-start
  19.2 19.9 %all_to_all.185 = f32[32,1,1536]{2,1,0:T(1,128)S(1)} all-to-all(f32[32,1,1536]{2,1,0:T(1,128)S(1)} %reshape.174), channel_id=1, replica_groups=mesh['samples'=4,'features'=32,'rhs'=2] {'features'}, dimensions={0} | all-to-all | bytes 393216 | tf_op jit(solution)/shard_map/all_to_all | solution.py:44
  41.9 4.1 all-to-all-start.3
  47.4 8.6 %all-to-all-done.3 = f32[32,1,1536]{2,1,0:T(1,128)S(1)} async-done(((f32[32,1,1536]{2,1,0:T(1,128)}), f32[32,1,1536]{2,1,0:T(1,128)S(1)}, u32[]{:S(2)}, u32[]{:S(2)}) %all-to-all-start.3) | async-done | bytes 196640 | tf_op jit(solution)/shard_map/all_to_all | solution.py:14
  58.3 6.0 convolution_bitcast_fusion.2
  65.5 3.9 all-to-all-start.4
  70.7 23.7 %all-to-all-done.4 = f32[32,128,64]{1,2,0:T(8,128)S(1)} async-done(((f32[32,128,64]{1,2,0:T(8,128)}), f32[32,128,64]{1,2,0:T(8,128)S(1)}, u32[]{:S(2)}, u32[]{:S(2)}) %all-to-all-start.4) | async-done | bytes 1048608 | tf_op jit(solution)/shard_map/all_to_all | solution.py:44
  94.4 6.7 all-to-all-start.9
  101.2 8.5 %all-to-all-done.9 = f32[32,1,128]{2,1,0:T(1,128)S(1)} async-done(((f32[32,1,128]{2,1,0:T(1,128)}), f32[32,1,128]{2,1,0:T(1,128)S(1)}, u32[]{:S(2)}, u32[]{:S(2)}) %all-to-all-start.9) | async-done | bytes 16416 | tf_op jit(solution)/shard_map/all_to_all | solution.py:44
  110.5 3.9 all-to-all-start.5
  116.0 11.4 %all-to-all-done.5 = bf16[32,128,64]{1,2,0:T(8,128)(2,1)S(1)} async-done(((bf16[32,128,64]{1,2,0:T(8,128)(2,1)}), bf16[32,128,64]{1,2,0:T(8,128)(2,1)S(1)}, u32[]{:S(2)}, u32[]{:S(2)}) %all-to-all-start.5) | async-done | bytes 524320 | tf_op jit(solution)/shard_map/all_to_all | solution.py:14
  127.3 5.9 all-to-all-start.10
  133.3 4.9 convolution_bitcast_fusion.5
  143.4 10.2 %all-to-all-start.6 = ((f32[8,1024,64]{1,2,0:T(8,128)}), f32[8,1024,64]{1,2,0:T(8,128)}, u32[]{:S(2)}, u32[]{:S(2)}) async-start(f32[8,1024,64]{1,2,0:T(8,128)} %broadcast_in_dim.47), calls=%async_computation.6 | async-start | bytes 4194304 | tf_op jit(solution)/shard_map/all_to_all | solution.py:14
  154.3 25.5 %all-to-all-done.6 = f32[8,1024,64]{1,2,0:T(8,128)} async-done(((f32[8,1024,64]{1,2,0:T(8,128)}), f32[8,1024,64]{1,2,0:T(8,128)}, u32[]{:S(2)}, u32[]{:S(2)}) %all-to-all-start.6) | async-done | bytes 2097184 | tf_op jit(solution)/shard_map/all_to_all | solution.py:14
  182.6 4.8 all-to-all-start.7
  188.7 7.2 %all-to-all-done.7 = f32[32,1,128]{2,1,0:T(1,128)S(1)} async-done(((f32[32,1,128]{2,1,0:T(1,128)}), f32[32,1,128]{2,1,0:T(1,128)S(1)}, u32[]{:S(2)}, u32[]{:S(2)}) %all-to-all-start.7) | async-done | bytes 16416 | tf_op jit(solution)/shard_map/all_to_all | solution.py:44
  200.9 7.5 %all-to-all-done.13 = f32[32,1,128]{2,1,0:T(1,128)S(1)} async-done(((f32[32,1,128]{2,1,0:T(1,128)}), f32[32,1,128]{2,1,0:T(1,128)S(1)}, u32[]{:S(2)}, u32[]{:S(2)}) %all-to-all-start.13) | async-done | bytes 16416 | tf_op jit(solution)/shard_map/all_to_all | solution.py:44
  214.3 6.5 all-to-all-done.15
  233.2 5.4 all-to-all-start.14
  239.6 5.8 cholesky.59
  247.2 8.2 %all-to-all-start.16 = ((f32[32,1,128]{2,1,0:T(1,128)}), f32[32,1,128]{2,1,0:T(1,128)S(1)}, u32[]{:S(2)}, u32[]{:S(2)}) async-start(f32[32,1,128]{2,1,0:T(1,128)} %reshape.196), calls=%async_computation.16 | async-start | bytes 32768 | tf_op jit(solution)/shard_map/all_to_all | solution.py:14
  256.0 4.9 custom-call.21
  263.9 7.6 %all-to-all-start.11 = ((f32[32,1,1536]{2,1,0:T(1,128)}), f32[32,1,1536]{2,1,0:T(1,128)S(1)}, u32[]{:S(2)}, u32[]{:S(2)}) async-start(f32[32,1,1536]{2,1,0:T(1,128)} %reshape.186), calls=%async_computation.11 | async-start | bytes 393216 | tf_op jit(solution)/shard_map/all_to_all | solution.py:44
  274.0 7.4 %all-to-all-done.11 = f32[32,1,1536]{2,1,0:T(1,128)S(1)} async-done(((f32[32,1,1536]{2,1,0:T(1,128)}), f32[32,1,1536]{2,1,0:T(1,128)S(1)}, u32[]{:S(2)}, u32[]{:S(2)}) %all-to-all-start.11) | async-done | bytes 196640 | tf_op jit(solution)/shard_map/all_to_all | solution.py:44
  283.6 4.1 all-to-all-start.12
  288.3 9.4 %all-to-all-done.12 = f32[32,1,1536]{2,1,0:T(1,128)S(1)} async-done(((f32[32,1,1536]{2,1,0:T(1,128)}), f32[32,1,1536]{2,1,0:T(1,128)S(1)}, u32[]{:S(2)}, u32[]{:S(2)}) %all-to-all-start.12) | async-done | bytes 196640 | tf_op jit(solution)/shard_map/all_to_all | solution.py:14
  301.9 6.0 convolution_bitcast_fusion.1
  309.1 3.9 all-to-all-start.17
  314.1 17.7 %all-to-all-done.17 = f32[32,128,64]{1,2,0:T(8,128)S(1)} async-done(((f32[32,128,64]{1,2,0:T(8,128)}), f32[32,128,64]{1,2,0:T(8,128)S(1)}, u32[]{:S(2)}, u32[]{:S(2)}) %all-to-all-start.17) | async-done | bytes 1048608 | tf_op jit(solution)/shard_map/all_to_all | solution.py:44
  331.8 6.8 all-to-all-start.22
  338.7 8.5 %all-to-all-done.22 = f32[32,1,128]{2,1,0:T(1,128)S(1)} async-done(((f32[32,1,128]{2,1,0:T(1,128)}), f32[32,1,128]{2,1,0:T(1,128)S(1)}, u32[]{:S(2)}, u32[]{:S(2)}) %all-to-all-start.22) | async-done | bytes 16416 | tf_op jit(solution)/shard_map/all_to_all | solution.py:44
  348.1 3.9 all-to-all-start.18
  353.5 11.4 %all-to-all-done.18 = bf16[32,128,64]{1,2,0:T(8,128)(2,1)S(1)} async-done(((bf16[32,128,64]{1,2,0:T(8,128)(2,1)}), bf16[32,128,64]{1,2,0:T(8,128)(2,1)S(1)}, u32[]{:S(2)}, u32[]{:S(2)}) %all-to-all-start.18) | async-done | bytes 524320 | tf_op jit(solution)/shard_map/all_to_all | solution.py:14
  368.7 4.9 convolution_bitcast_fusion.4
  378.8 16.9 %all-to-all-start.19 = ((f32[8,1024,64]{1,2,0:T(8,128)}), f32[8,1024,64]{1,2,0:T(8,128)}, u32[]{:S(2)}, u32[]{:S(2)}) async-start(f32[8,1024,64]{1,2,0:T(8,128)} %broadcast_in_dim.54), calls=%async_computation.19 | async-start | bytes 4194304 | tf_op jit(solution)/shard_map/all_to_all | solution.py:14
  396.5 25.6 %all-to-all-done.19 = f32[8,1024,64]{1,2,0:T(8,128)} async-done(((f32[8,1024,64]{1,2,0:T(8,128)}), f32[8,1024,64]{1,2,0:T(8,128)}, u32[]{:S(2)}, u32[]{:S(2)}) %all-to-all-start.19) | async-done | bytes 2097184 | tf_op jit(solution)/shard_map/all_to_all | solution.py:14
  424.9 4.8 all-to-all-start.20
  430.8 7.5 %all-to-all-done.20 = f32[32,1,128]{2,1,0:T(1,128)S(1)} async-done(((f32[32,1,128]{2,1,0:T(1,128)}), f32[32,1,128]{2,1,0:T(1,128)S(1)}, u32[]{:S(2)}, u32[]{:S(2)}) %all-to-all-start.20) | async-done | bytes 16416 | tf_op jit(solution)/shard_map/all_to_all | solution.py:44
  443.2 7.5 %all-to-all-done.26 = f32[32,1,128]{2,1,0:T(1,128)S(1)} async-done(((f32[32,1,128]{2,1,0:T(1,128)}), f32[32,1,128]{2,1,0:T(1,128)S(1)}, u32[]{:S(2)}, u32[]{:S(2)}) %all-to-all-start.26) | async-done | bytes 16416 | tf_op jit(solution)/shard_map/all_to_all | solution.py:44
  450.7 4.3 all-to-all-start.28
  457.1 6.5 all-to-all-done.28
  475.9 5.4 all-to-all-start.27
  482.3 5.8 cholesky.70
  489.5 4.9 custom-call.26
  494.4 9.2 %all-to-all-start.29 = ((f32[32,1,128]{2,1,0:T(1,128)}), f32[32,1,128]{2,1,0:T(1,128)S(1)}, u32[]{:S(2)}, u32[]{:S(2)}) async-start(f32[32,1,128]{2,1,0:T(1,128)} %reshape.216), calls=%async_computation.29 | async-start | bytes 32768 | tf_op jit(solution)/shard_map/all_to_all | solution.py:14
  504.8 7.4 %all-to-all-done.29 = f32[32,1,128]{2,1,0:T(1,128)S(1)} async-done(((f32[32,1,128]{2,1,0:T(1,128)}), f32[32,1,128]{2,1,0:T(1,128)S(1)}, u32[]{:S(2)}, u32[]{:S(2)}) %all-to-all-start.29) | async-done | bytes 16416 | tf_op jit(solution)/shard_map/all_to_all | solution.py:14
  517.6 8.5 %all-to-all-done.24 = f32[32,1,1536]{2,1,0:T(1,128)S(1)} async-done(((f32[32,1,1536]{2,1,0:T(1,128)}), f32[32,1,1536]{2,1,0:T(1,128)S(1)}, u32[]{:S(2)}, u32[]{:S(2)}) %all-to-all-start.24) | async-done | bytes 196640 | tf_op jit(solution)/shard_map/all_to_all | solution.py:44
  528.3 4.0 all-to-all-start.25
  533.0 9.4 %all-to-all-done.25 = f32[32,1,1536]{2,1,0:T(1,128)S(1)} async-done(((f32[32,1,1536]{2,1,0:T(1,128)}), f32[32,1,1536]{2,1,0:T(1,128)S(1)}, u32[]{:S(2)}, u32[]{:S(2)}) %all-to-all-start.25) | async-done | bytes 196640 | tf_op jit(solution)/shard_map/all_to_all | solution.py:14
  546.6 6.0 convolution_bitcast_fusion
  552.7 21.3 %all_to_all.186 = f32[32,128,64]{1,2,0:T(8,128)S(1)} all-to-all(f32[32,128,64]{1,2,0:T(8,128)S(1)} %bitcast.295), channel_id=1, replica_groups=mesh['samples'=4,'features'=32,'rhs'=2] {'features'}, dimensions={0} | all-to-all | bytes 2097152 | tf_op jit(solution)/shard_map/all_to_all | solution.py:44
  574.2 19.3 %all_to_all.187 = bf16[32,128,64]{1,2,0:T(8,128)(2,1)S(1)} all-to-all(bf16[32,128,64]{1,2,0:T(8,128)(2,1)S(1)} %broadcast_in_dim.60), channel_id=1, replica_groups=mesh['samples'=4,'features'=32,'rhs'=2] {'features'}, dimensions={0} | all-to-all | bytes 1048576 | tf_op jit(solution)/shard_map/all_to_all | solution.py:14
  593.5 5.0 convolution_bitcast_fusion.3
  600.1 14.2 %all-to-all-start.32 = ((f32[8,1024,64]{1,2,0:T(8,128)}), f32[8,1024,64]{1,2,0:T(8,128)S(1)}, u32[]{:S(2)}, u32[]{:S(2)}) async-start(f32[8,1024,64]{1,2,0:T(8,128)} %broadcast_in_dim.61), calls=%async_computation.32 | async-start | bytes 4194304 | tf_op jit(solution)/shard_map/all_to_all | solution.py:14
  615.3 25.2 %all-to-all-done.32 = f32[8,1024,64]{1,2,0:T(8,128)S(1)} async-done(((f32[8,1024,64]{1,2,0:T(8,128)}), f32[8,1024,64]{1,2,0:T(8,128)S(1)}, u32[]{:S(2)}, u32[]{:S(2)}) %all-to-all-start.32) | async-done | bytes 2097184 | tf_op jit(solution)/shard_map/all_to_all | solution.py:14
  640.5 4.1 all-to-all-start.35
  645.8 7.3 %all-to-all-done.35 = f32[32,1,128]{2,1,0:T(1,128)S(1)} async-done(((f32[32,1,128]{2,1,0:T(1,128)}), f32[32,1,128]{2,1,0:T(1,128)S(1)}, u32[]{:S(2)}, u32[]{:S(2)}) %all-to-all-start.35) | async-done | bytes 16416 | tf_op jit(solution)/shard_map/all_to_all | solution.py:44
  658.5 7.0 all-to-all-done.33
  671.3 6.6 all-to-all-done.36
  677.9 4.0 all-to-all-start.34
  683.2 7.4 %all-to-all-done.34 = f32[32,1,128]{2,1,0:T(1,128)S(1)} async-done(((f32[32,1,128]{2,1,0:T(1,128)}), f32[32,1,128]{2,1,0:T(1,128)S(1)}, u32[]{:S(2)}, u32[]{:S(2)}) %all-to-all-start.34) | async-done | bytes 16416 | tf_op jit(solution)/shard_map/all_to_all | solution.py:14
  691.5 5.8 cholesky.81
  698.7 4.9 custom-call.31
  (248 shorter events, 146.1 us)
Async XLA Ops:
  2.2 8.0 %all-to-all-start = ((f32[2,1024,32]{1,2,0:T(8,128)}), f32[2,1024,32]{1,2,0:T(8,128)S(1)}, u32[]{:S(2)}, u32[]{:S(2)}) async-start(f32[2,1024,32]{1,2,0:T(8,128)} %broadcast_in_dim.43), calls=%async_computation | async-start | bytes 524288 | tf_op jit(solution)/shard_map/all_to_all | solution.py:14
  11.6 5.9 all-to-all-start.1
  19.2 26.8 %copy-start.8 = (f32[768]{0:T(1024)S(1)}, f32[768]{0:T(1024)}, u32[]{:S(2)}) copy-start(f32[768]{0:T(1024)} %param.14) | copy-start | bytes 9220
  41.9 14.0 %all-to-all-start.3 = ((f32[32,1,1536]{2,1,0:T(1,128)}), f32[32,1,1536]{2,1,0:T(1,128)S(1)}, u32[]{:S(2)}, u32[]{:S(2)}) async-start(f32[32,1,1536]{2,1,0:T(1,128)} %reshape.176), calls=%async_computation.3 | async-start | bytes 393216 | tf_op jit(solution)/shard_map/all_to_all | solution.py:14
  57.9 6.5 copy-start.2
  65.5 28.9 %all-to-all-start.4 = ((f32[32,128,64]{1,2,0:T(8,128)}), f32[32,128,64]{1,2,0:T(8,128)S(1)}, u32[]{:S(2)}, u32[]{:S(2)}) async-start(f32[32,128,64]{1,2,0:T(8,128)} %bitcast.293), calls=%async_computation.4 | async-start | bytes 2097152 | tf_op jit(solution)/shard_map/all_to_all | solution.py:44
  94.4 15.2 %all-to-all-start.9 = ((f32[32,1,128]{2,1,0:T(1,128)}), f32[32,1,128]{2,1,0:T(1,128)S(1)}, u32[]{:S(2)}, u32[]{:S(2)}) async-start(f32[32,1,128]{2,1,0:T(1,128)} %reshape.182), calls=%async_computation.9 | async-start | bytes 32768 | tf_op jit(solution)/shard_map/all_to_all | solution.py:44
  110.5 16.8 %all-to-all-start.5 = ((bf16[32,128,64]{1,2,0:T(8,128)(2,1)}), bf16[32,128,64]{1,2,0:T(8,128)(2,1)S(1)}, u32[]{:S(2)}, u32[]{:S(2)}) async-start(bf16[32,128,64]{1,2,0:T(8,128)(2,1)} %broadcast_in_dim.46), calls=%async_computation.5 | async-start | bytes 1048576 | tf_op jit(solution)/shard_map/all_to_all | solution.py:14
  127.3 14.5 %all-to-all-start.10 = ((f32[32,1,128]{2,1,0:T(1,128)}), f32[32,1,128]{2,1,0:T(1,128)S(1)}, u32[]{:S(2)}, u32[]{:S(2)}) async-start(f32[32,1,128]{2,1,0:T(1,128)} %reshape.184), calls=%async_computation.10 | async-start | bytes 32768 | tf_op jit(solution)/shard_map/all_to_all | solution.py:14
  143.4 36.4 %all-to-all-start.6 = ((f32[8,1024,64]{1,2,0:T(8,128)}), f32[8,1024,64]{1,2,0:T(8,128)}, u32[]{:S(2)}, u32[]{:S(2)}) async-start(f32[8,1024,64]{1,2,0:T(8,128)} %broadcast_in_dim.47), calls=%async_computation.6 | async-start | bytes 4194304 | tf_op jit(solution)/shard_map/all_to_all | solution.py:14
  182.6 13.3 %all-to-all-start.7 = ((f32[32,1,128]{2,1,0:T(1,128)}), f32[32,1,128]{2,1,0:T(1,128)S(1)}, u32[]{:S(2)}, u32[]{:S(2)}) async-start(f32[32,1,128]{2,1,0:T(1,128)} %reshape.178), calls=%async_computation.7 | async-start | bytes 32768 | tf_op jit(solution)/shard_map/all_to_all | solution.py:44
  196.0 12.4 %all-to-all-start.13 = ((f32[32,1,128]{2,1,0:T(1,128)}), f32[32,1,128]{2,1,0:T(1,128)S(1)}, u32[]{:S(2)}, u32[]{:S(2)}) async-start(f32[32,1,128]{2,1,0:T(1,128)} %reshape.190), calls=%async_computation.13 | async-start | bytes 32768 | tf_op jit(solution)/shard_map/all_to_all | solution.py:44
  208.3 12.5 %all-to-all-start.15 = ((f32[32,1,128]{2,1,0:T(1,128)}), f32[32,1,128]{2,1,0:T(1,128)S(1)}, u32[]{:S(2)}, u32[]{:S(2)}) async-start(f32[32,1,128]{2,1,0:T(1,128)} %reshape.194), calls=%async_computation.15 | async-start | bytes 32768 | tf_op jit(solution)/shard_map/all_to_all | solution.py:44
  220.8 12.4 %all-to-all-start.8 = ((f32[32,1,128]{2,1,0:T(1,128)}), f32[32,1,128]{2,1,0:T(1,128)S(1)}, u32[]{:S(2)}, u32[]{:S(2)}) async-start(f32[32,1,128]{2,1,0:T(1,128)} %reshape.180), calls=%async_computation.8 | async-start | bytes 32768 | tf_op jit(solution)/shard_map/all_to_all | solution.py:14
  233.2 14.0 %all-to-all-start.14 = ((f32[32,1,128]{2,1,0:T(1,128)}), f32[32,1,128]{2,1,0:T(1,128)S(1)}, u32[]{:S(2)}, u32[]{:S(2)}) async-start(f32[32,1,128]{2,1,0:T(1,128)} %reshape.192), calls=%async_computation.14 | async-start | bytes 32768 | tf_op jit(solution)/shard_map/all_to_all | solution.py:14
  247.2 16.8 %all-to-all-start.16 = ((f32[32,1,128]{2,1,0:T(1,128)}), f32[32,1,128]{2,1,0:T(1,128)S(1)}, u32[]{:S(2)}, u32[]{:S(2)}) async-start(f32[32,1,128]{2,1,0:T(1,128)} %reshape.196), calls=%async_computation.16 | async-start | bytes 32768 | tf_op jit(solution)/shard_map/all_to_all | solution.py:14
  263.9 17.4 %all-to-all-start.11 = ((f32[32,1,1536]{2,1,0:T(1,128)}), f32[32,1,1536]{2,1,0:T(1,128)S(1)}, u32[]{:S(2)}, u32[]{:S(2)}) async-start(f32[32,1,1536]{2,1,0:T(1,128)} %reshape.186), calls=%async_computation.11 | async-start | bytes 393216 | tf_op jit(solution)/shard_map/all_to_all | solution.py:44
  273.3 28.2 %copy-start.4 = (f32[64,1024]{1,0:T(8,128)}, f32[64,1024]{1,0:T(8,128)S(1)}, u32[]{:S(2)}) copy-start(f32[64,1024]{1,0:T(8,128)S(1)} %fusion.64) | copy-start | bytes 786436
  282.7 16.2 %copy-start.3 = (f32[768,64]{0,1:T(8,128)S(1)}, f32[768,64]{0,1:T(8,128)}, u32[]{:S(2)}) copy-start(f32[768,64]{0,1:T(8,128)} %copy-done.2) | copy-start | bytes 589828
  283.6 14.0 %all-to-all-start.12 = ((f32[32,1,1536]{2,1,0:T(1,128)}), f32[32,1,1536]{2,1,0:T(1,128)S(1)}, u32[]{:S(2)}, u32[]{:S(2)}) async-start(f32[32,1,1536]{2,1,0:T(1,128)} %reshape.188), calls=%async_computation.12 | async-start | bytes 393216 | tf_op jit(solution)/shard_map/all_to_all | solution.py:14
  298.9 1.8 copy-start.6
  298.9 1.8 copy-start.7
  299.5 2.0 copy-start
  309.1 22.7 %all-to-all-start.17 = ((f32[32,128,64]{1,2,0:T(8,128)}), f32[32,128,64]{1,2,0:T(8,128)S(1)}, u32[]{:S(2)}, u32[]{:S(2)}) async-start(f32[32,128,64]{1,2,0:T(8,128)} %bitcast.294), calls=%async_computation.17 | async-start | bytes 2097152 | tf_op jit(solution)/shard_map/all_to_all | solution.py:44
  331.8 15.3 %all-to-all-start.22 = ((f32[32,1,128]{2,1,0:T(1,128)}), f32[32,1,128]{2,1,0:T(1,128)S(1)}, u32[]{:S(2)}, u32[]{:S(2)}) async-start(f32[32,1,128]{2,1,0:T(1,128)} %reshape.202), calls=%async_computation.22 | async-start | bytes 32768 | tf_op jit(solution)/shard_map/all_to_all | solution.py:44
  348.1 16.8 %all-to-all-start.18 = ((bf16[32,128,64]{1,2,0:T(8,128)(2,1)}), bf16[32,128,64]{1,2,0:T(8,128)(2,1)S(1)}, u32[]{:S(2)}, u32[]{:S(2)}) async-start(bf16[32,128,64]{1,2,0:T(8,128)(2,1)} %broadcast_in_dim.53), calls=%async_computation.18 | async-start | bytes 1048576 | tf_op jit(solution)/shard_map/all_to_all | solution.py:14
  364.9 12.4 %all-to-all-start.23 = ((f32[32,1,128]{2,1,0:T(1,128)}), f32[32,1,128]{2,1,0:T(1,128)S(1)}, u32[]{:S(2)}, u32[]{:S(2)}) async-start(f32[32,1,128]{2,1,0:T(1,128)} %reshape.204), calls=%async_computation.23 | async-start | bytes 32768 | tf_op jit(solution)/shard_map/all_to_all | solution.py:14
  378.8 43.3 %all-to-all-start.19 = ((f32[8,1024,64]{1,2,0:T(8,128)}), f32[8,1024,64]{1,2,0:T(8,128)}, u32[]{:S(2)}, u32[]{:S(2)}) async-start(f32[8,1024,64]{1,2,0:T(8,128)} %broadcast_in_dim.54), calls=%async_computation.19 | async-start | bytes 4194304 | tf_op jit(solution)/shard_map/all_to_all | solution.py:14
  424.9 13.3 %all-to-all-start.20 = ((f32[32,1,128]{2,1,0:T(1,128)}), f32[32,1,128]{2,1,0:T(1,128)S(1)}, u32[]{:S(2)}, u32[]{:S(2)}) async-start(f32[32,1,128]{2,1,0:T(1,128)} %reshape.198), calls=%async_computation.20 | async-start | bytes 32768 | tf_op jit(solution)/shard_map/all_to_all | solution.py:44
  438.3 12.4 %all-to-all-start.26 = ((f32[32,1,128]{2,1,0:T(1,128)}), f32[32,1,128]{2,1,0:T(1,128)S(1)}, u32[]{:S(2)}, u32[]{:S(2)}) async-start(f32[32,1,128]{2,1,0:T(1,128)} %reshape.210), calls=%async_computation.26 | async-start | bytes 32768 | tf_op jit(solution)/shard_map/all_to_all | solution.py:44
  450.7 12.9 %all-to-all-start.28 = ((f32[32,1,128]{2,1,0:T(1,128)}), f32[32,1,128]{2,1,0:T(1,128)S(1)}, u32[]{:S(2)}, u32[]{:S(2)}) async-start(f32[32,1,128]{2,1,0:T(1,128)} %reshape.214), calls=%async_computation.28 | async-start | bytes 32768 | tf_op jit(solution)/shard_map/all_to_all | solution.py:44
  463.5 12.4 %all-to-all-start.21 = ((f32[32,1,128]{2,1,0:T(1,128)}), f32[32,1,128]{2,1,0:T(1,128)S(1)}, u32[]{:S(2)}, u32[]{:S(2)}) async-start(f32[32,1,128]{2,1,0:T(1,128)} %reshape.200), calls=%async_computation.21 | async-start | bytes 32768 | tf_op jit(solution)/shard_map/all_to_all | solution.py:14
  475.9 18.5 %all-to-all-start.27 = ((f32[32,1,128]{2,1,0:T(1,128)}), f32[32,1,128]{2,1,0:T(1,128)S(1)}, u32[]{:S(2)}, u32[]{:S(2)}) async-start(f32[32,1,128]{2,1,0:T(1,128)} %reshape.212), calls=%async_computation.27 | async-start | bytes 32768 | tf_op jit(solution)/shard_map/all_to_all | solution.py:14
  494.4 17.9 %all-to-all-start.29 = ((f32[32,1,128]{2,1,0:T(1,128)}), f32[32,1,128]{2,1,0:T(1,128)S(1)}, u32[]{:S(2)}, u32[]{:S(2)}) async-start(f32[32,1,128]{2,1,0:T(1,128)} %reshape.216), calls=%async_computation.29 | async-start | bytes 32768 | tf_op jit(solution)/shard_map/all_to_all | solution.py:14
  512.3 13.8 %all-to-all-start.24 = ((f32[32,1,1536]{2,1,0:T(1,128)}), f32[32,1,1536]{2,1,0:T(1,128)S(1)}, u32[]{:S(2)}, u32[]{:S(2)}) async-start(f32[32,1,1536]{2,1,0:T(1,128)} %reshape.206), calls=%async_computation.24 | async-start | bytes 393216 | tf_op jit(solution)/shard_map/all_to_all | solution.py:44
  527.4 16.2 %copy-start.1 = (f32[768,64]{0,1:T(8,128)S(1)}, f32[768,64]{0,1:T(8,128)}, u32[]{:S(2)}) copy-start(f32[768,64]{0,1:T(8,128)} %copy-done) | copy-start | bytes 589828
  528.3 14.0 %all-to-all-start.25 = ((f32[32,1,1536]{2,1,0:T(1,128)}), f32[32,1,1536]{2,1,0:T(1,128)S(1)}, u32[]{:S(2)}, u32[]{:S(2)}) async-start(f32[32,1,1536]{2,1,0:T(1,128)} %reshape.208), calls=%async_computation.25 | async-start | bytes 393216 | tf_op jit(solution)/shard_map/all_to_all | solution.py:14
  600.1 40.4 %all-to-all-start.32 = ((f32[8,1024,64]{1,2,0:T(8,128)}), f32[8,1024,64]{1,2,0:T(8,128)S(1)}, u32[]{:S(2)}, u32[]{:S(2)}) async-start(f32[8,1024,64]{1,2,0:T(8,128)} %broadcast_in_dim.61), calls=%async_computation.32 | async-start | bytes 4194304 | tf_op jit(solution)/shard_map/all_to_all | solution.py:14
  640.5 12.6 %all-to-all-start.35 = ((f32[32,1,128]{2,1,0:T(1,128)}), f32[32,1,128]{2,1,0:T(1,128)S(1)}, u32[]{:S(2)}, u32[]{:S(2)}) async-start(f32[32,1,128]{2,1,0:T(1,128)} %reshape.222), calls=%async_computation.35 | async-start | bytes 32768 | tf_op jit(solution)/shard_map/all_to_all | solution.py:44
  644.6 24.8 %copy-start.5 = (f32[64,1024]{1,0:T(8,128)S(1)}, f32[64,1024]{1,0:T(8,128)}, u32[]{:S(2)}) copy-start(f32[64,1024]{1,0:T(8,128)} %copy-done.4) | copy-start | bytes 786436
  653.1 12.4 %all-to-all-start.33 = ((f32[32,1,128]{2,1,0:T(1,128)}), f32[32,1,128]{2,1,0:T(1,128)S(1)}, u32[]{:S(2)}, u32[]{:S(2)}) async-start(f32[32,1,128]{2,1,0:T(1,128)} %reshape.218), calls=%async_computation.33 | async-start | bytes 32768 | tf_op jit(solution)/shard_map/all_to_all | solution.py:44
  665.5 12.4 %all-to-all-start.36 = ((f32[32,1,128]{2,1,0:T(1,128)}), f32[32,1,128]{2,1,0:T(1,128)S(1)}, u32[]{:S(2)}, u32[]{:S(2)}) async-start(f32[32,1,128]{2,1,0:T(1,128)} %reshape.224), calls=%async_computation.36 | async-start | bytes 32768 | tf_op jit(solution)/shard_map/all_to_all | solution.py:14
  677.9 12.6 %all-to-all-start.34 = ((f32[32,1,128]{2,1,0:T(1,128)}), f32[32,1,128]{2,1,0:T(1,128)S(1)}, u32[]{:S(2)}, u32[]{:S(2)}) async-start(f32[32,1,128]{2,1,0:T(1,128)} %reshape.220), calls=%async_computation.34 | async-start | bytes 32768 | tf_op jit(solution)/shard_map/all_to_all | solution.py:14
where the time goes:
time: 721 us; the launch traced here: 706 us
  waiting for transfers between devices  298 us (41%)
  starting transfers between devices  191 us (26%)
  other arithmetic  62.4 us (9%)
  blocking collectives  60.5 us (8%)
  matrix products  53 us (7%)
  local copies, waits for them, and re-layouts  38.2 us (5%)
    all_to_all x20, waiting for transfers between devices, sent_to_all(): lax.all_to_all(jnp.broadcast_to(array[None], (size, *array.shape)), axis,...  167 us
    all_to_all x14, waiting for transfers between devices, summed_on_arrival(): lax.all_to_all(parts, axis, split_axis=0, concat_axis=0, tiled=True)  131 us
    all_to_all x20, starting transfers between devices, sent_to_all(): lax.all_to_all(jnp.broadcast_to(array[None], (size, *array.shape)), axis,...  125 us
    all_to_all x14, starting transfers between devices, summed_on_arrival(): lax.all_to_all(parts, axis, split_axis=0, concat_axis=0, tiled=True)  66 us
    all_to_all x2, blocking collectives, summed_on_arrival(): lax.all_to_all(parts, axis, split_axis=0, concat_axis=0, tiled=True)  41.2 us
    unnamed x71, local copies, waits for them, and re-layouts  23.9 us
    another operation x9, other arithmetic, shards(): chol_lower = jnp.linalg.cholesky(gram_block)  19.6 us
    all_to_all x1, blocking collectives, sent_to_all(): lax.all_to_all(jnp.broadcast_to(array[None], (size, *array.shape)), axis,...  19.3 us
  transfers between devices with their start and end apart: 34, of which 32 were waited for; matrix products, arithmetic and copies ran while one was open for 11% of the time, Pallas kernels for 0%

commit v1 on v0

v1 whole, which is shorter than its diff:
```python
import functools

import jax
import jax.numpy as jnp
from jax import lax
from jax.experimental import pallas as pl
from jax.experimental.pallas import tpu as pltpu
from jax.sharding import PartitionSpec as P

ITERS = 3
LANES = 128
MESH = pl.DeviceIdType.MESH
F32 = jnp.float32
BF16 = jnp.bfloat16
WIRE = jnp.float32


def nt(a, b):
    return lax.dot_general(a, b, (((1,), (1,)), ((), ())), preferred_element_type=F32)


def nn(a, b):
    return lax.dot_general(a, b, (((1,), (0,)), ((), ())), preferred_element_type=F32)


def halves(v):
    upper = v.astype(BF16)
    lower = (v - upper.astype(F32)).astype(BF16)
    return upper, lower


def nn_fine(a, b):
    ah, al = halves(a)
    bh, bl = halves(b)
    return nn(jnp.concatenate([ah, ah, al, al], 1), jnp.concatenate([bh, bl, bh, bl], 0))


def nt_fine(a, b):
    m, n = a.shape[0], b.shape[0]
    t = nt(jnp.concatenate(halves(a), 0), jnp.concatenate(halves(b), 0))
    return t[:m, :n] + t[:m, n:] + t[m:, :n] + t[m:, n:]


def rows_fine(a, op, b):
    m = a.shape[0]
    t = op(jnp.concatenate(halves(a), 0), b)
    return t[:m] + t[m:]


def inverse(a):
    n = a.shape[0]
    lane = lax.broadcasted_iota(jnp.int32, (1, n), 1)
    sub = lax.broadcasted_iota(jnp.int32, (n, 1), 0)
    for i in range(n):
        pivot = 1.0 / a[i : i + 1, i : i + 1]
        row = jnp.where(lane == i, 1.0, a[i : i + 1, :]) * pivot
        col = a[:, i : i + 1]
        rest = jnp.where(lane == i, 0.0, a) - col * row
        a = jnp.where(sub == i, row, rest)
    return a


def kernel(
    dims,
    d_hbm, rt_in, f_in, shrink,
    x_out, r_out,
    dv, rfull, fall, pt, rt, xt, yt, ginv, qt,
    s1, r1, acc1, s2, r2, own2, img, qacc,
    gxs, gxr, gyr, gzr, gall,
    qds, qdr, qxr, qf,
    wyr, wzr, wall,
    dsem, rsem, fsem,
    s1s, s1r, s2s, s2r, izs, izr, iys, iyr,
    gxss, gxsr, gyss, gysr, gzss, gzsr, gass, gasr,
    qdsem, qxss, qxsr, qfsem,
    wyss, wysr, wzss, wzsr, wxss, wxsr,
):
    nx, nc, nz, ny, iters = dims
    nxc, npair, nblk = nx * nc, nz // 2, nx - 1
    k = pt.shape[0]
    feats = pt.shape[1]
    half = feats // nc
    rank_half = f_in.shape[1]
    rows = dv.shape[0] // ny
    x, f, c = lax.axis_index("samples"), lax.axis_index("features"), lax.axis_index("rhs")
    z, y = lax.div(f, ny), lax.rem(f, ny)
    other = 1 - c
    j = c * nx + x

    def to_y(yy):
        return {"features": z * ny + yy}

    def to_z(zz):
        return {"features": zz * ny + y}

    def to_core():
        return {"rhs": other}

    def to_x(xx):
        return {"samples": xx}

    def to_j(jj):
        return {"samples": lax.rem(jj, nx), "rhs": lax.div(jj, nx)}

    def copy(src, dst, ss, rs, dev):
        return pltpu.make_async_remote_copy(
            src_ref=src, dst_ref=dst, send_sem=ss, recv_sem=rs, device_id=dev, device_id_type=MESH
        )

    def start_all(ref, me, n, to, ss, rs):
        for d in range(1, n):
            other_one = lax.rem(me + d, n)
            copy(ref.at[me], ref.at[me], ss.at[d], rs.at[me], to(other_one)).start()

    def wait_all(ref, me, n, to, ss, rs):
        for d in range(1, n):
            other_one = lax.rem(me + d, n)
            copy(ref.at[other_one], ref.at[other_one], ss.at[d], rs.at[other_one], to(other_one)).wait_recv()

    def sent_all(ref, me, n, to, ss, rs):
        for d in range(1, n):
            other_one = lax.rem(me + d, n)
            copy(ref.at[me], ref.at[me], ss.at[d], rs.at[me], to(other_one)).wait_send()

    def total(ref, n):
        t = ref[0].astype(F32)
        for i in range(1, n):
            t = t + ref[i].astype(F32)
        return t

    loads = [
        pltpu.make_async_copy(d_hbm.at[pl.ds(i * rows, rows)], dv.at[pl.ds(i * rows, rows)], dsem.at[i])
        for i in range(ny)
    ]
    for load in loads:
        load.start()

    barrier = pltpu.get_barrier_semaphore()
    for d in range(1, ny):
        pl.semaphore_signal(barrier, inc=1, device_id=to_y(lax.rem(y + d, ny)), device_id_type=MESH)
    for d in range(1, nz):
        pl.semaphore_signal(barrier, inc=1, device_id=to_z(lax.rem(z + d, nz)), device_id_type=MESH)
    for d in range(1, nxc):
        pl.semaphore_signal(barrier, inc=1, device_id=to_j(lax.rem(j + d, nxc)), device_id_type=MESH)
    pl.semaphore_wait(barrier, ny + nz + nxc - 3)

    send_r = copy(rt_in, rfull.at[c], rsem.at[0], rsem.at[1], to_core())
    send_r.start()
    send_f = copy(f_in, fall.at[c], fsem.at[0], fsem.at[1], to_core())
    send_f.start()
    rfull[c] = rt_in[...]
    fall[c] = f_in[...]

    def plane_start(value):
        wyr[y] = value.astype(WIRE)
        start_all(wyr, y, ny, to_y, wyss, wysr)

    def plane_finish():
        wait_all(wyr, y, ny, to_y, wyss, wysr)
        wzr[z] = total(wyr, ny).astype(WIRE)
        start_all(wzr, z, nz, to_z, wzss, wzsr)
        sent_all(wyr, y, ny, to_y, wyss, wysr)
        wait_all(wzr, z, nz, to_z, wzss, wzsr)
        wall[j] = total(wzr, nz).astype(WIRE)
        start_all(wall, j, nxc, to_j, wxss, wxsr)
        sent_all(wzr, z, nz, to_z, wzss, wzsr)
        wait_all(wall, j, nxc, to_j, wxss, wxsr)
        sent_all(wall, j, nxc, to_j, wxss, wxsr)

    def gathered():
        return jnp.concatenate([wall[cc * nx + b].astype(F32) for cc in range(nc) for b in range(nblk)], 1)

    def own_block(value):
        return rows_fine(value, nn, f_in[:, pl.ds(pl.multiple_of(x * LANES, LANES), LANES)])

    def spread(scaled):
        out = rows_fine(scaled[:, :rank_half], nt, fall[0])
        return out + rows_fine(scaled[:, rank_half:], nt, fall[1])

    copy(rt_in, rfull.at[other], rsem.at[0], rsem.at[1], to_core()).wait_recv()
    rt[...] = rfull[...].reshape(k, feats)
    xt[...] = jnp.zeros_like(xt)

    @pl.when(x < nblk)
    def _():
        plane_start(own_block(rt[...]))

    @pl.when(x == nblk)
    def _():
        plane_start(jnp.zeros((k, LANES), F32))

    plane_finish()
    copy(f_in, fall.at[other], fsem.at[0], fsem.at[1], to_core()).wait_recv()
    send_r.wait_send()
    send_f.wait_send()
    yt[...] = gathered()
    pt[...] = rt[...] + spread(yt[...] * shrink[...])
    for load in loads:
        load.wait()

    y_order = [d for d in (2, 1, 3) if d < ny]
    z_order = [d for d in (1, 7, 2, 6, 3, 5, 4) if d < nz]
    pair_order = [(npair // 2 + s) % npair for s in (0, 3, 1, 2)][:npair] if npair == 4 else list(range(1, npair)) + [0]
    pair_order = [p for p in pair_order if p] + [0]
    zq, zb = lax.div(z, 2), lax.rem(z, 2)
    mate = z + 1 - 2 * zb

    def s1_copy(d, p):
        return copy(s1.at[d - 1, p], r1.at[ny - d - 1, p], s1s.at[d - 1, p], s1r.at[ny - d - 1, p], to_y(lax.rem(y + d, ny)))

    def r1_copy(d, p):
        return copy(s1.at[d - 1, p], r1.at[d - 1, p], s1s.at[d - 1, p], s1r.at[d - 1, p], to_y(lax.rem(y + d, ny)))

    def s2_copy(slot, b, zz):
        return copy(s2.at[slot, b], r2.at[z], s2s.at[slot, b], s2r.at[z], to_z(zz))

    def iy_copy(d, zz, zslot):
        return copy(img.at[y, zz], img.at[y, zz], iys.at[d, zslot], iyr.at[y, zz], to_y(lax.rem(y + d, ny)))

    def iteration(step, carry):
        narrow = pt[...].astype(BF16)
        for p, off in enumerate(pair_order):
            q = lax.rem(zq + off, npair)
            for d in [*y_order, 0]:
                base = lax.rem(y + d, ny) * rows + q * (2 * LANES)
                part = nt(narrow, dv[pl.ds(pl.multiple_of(base, 2 * LANES), 2 * LANES), :])
                if d:
                    s1[d - 1, p] = part.astype(BF16)
                    s1_copy(d, p).start()
                else:
                    acc1[p] = part
        for p, off in enumerate(pair_order):
            tot = acc1[p]
            for d in range(1, ny):
                r1_copy(d, p).wait_recv()
                tot = tot + r1[d - 1, p].astype(F32)
            if off:
                q = lax.rem(zq + off, npair)
                for b in range(2):
                    s2[p, b] = tot[:, b * LANES : (b + 1) * LANES].astype(BF16)
                    s2_copy(p, b, 2 * q + b).start()
            else:
                own2[0] = tot[:, :LANES]
                own2[1] = tot[:, LANES:]
                s2[p, 0] = own2[1 - zb].astype(BF16)
                s2_copy(p, 0, mate).start()
        mine = own2[zb]
        for d in range(1, nz):
            zz = lax.rem(z + d, nz)
            copy(s2.at[0, 0], r2.at[zz], s2s.at[0, 0], s2r.at[zz], to_z(zz)).wait_recv()
            mine = mine + r2[zz].astype(F32)

        img[y, z] = mine.astype(BF16)
        for d in z_order:
            zz = lax.rem(z + d, nz)
            copy(img.at[y, z], img.at[y, z], izs.at[d], izr.at[z], to_z(zz)).start()
        for d in y_order:
            iy_copy(d, z, 0).start()

        lanes = pl.ds(pl.multiple_of(j * LANES, LANES), LANES)
        p_own, r_own = pt[:, lanes], rt[:, lanes]
        both = jnp.concatenate([mine, p_own], 1)
        gc = jnp.concatenate([nt_fine(both, both), nt_fine(r_own, p_own)], 1)
        gxs[...] = gc.reshape(gxs.shape)
        for d in range(1, nxc):
            jj = lax.rem(j + d, nxc)
            copy(gxs.at[jj], gxr.at[j], gxss.at[d], gxsr.at[j], to_j(jj)).start()
        gxr[j] = gxs[j]

        def forward(d):
            zz = lax.rem(z + d, nz)
            copy(img.at[y, zz], img.at[y, zz], izs.at[d], izr.at[zz], to_z(zz)).wait_recv()
            for e in y_order:
                iy_copy(e, zz, d).start()

        def project(yy):
            flat = jnp.concatenate([img[yy, zz] for zz in range(nz)], 1)
            return nn(flat, dv[pl.ds(pl.multiple_of(yy * rows, rows), rows), :])

        for d in z_order[:4]:
            forward(d)
        wait_all(gxr, j, nxc, to_j, gxss, gxsr)
        gyr[y] = total(gxr, nxc)
        start_all(gyr, y, ny, to_y, gyss, gysr)
        for d in z_order[4:]:
            forward(d)
        qacc[...] = project(y)
        wait_all(gyr, y, ny, to_y, gyss, gysr)
        gzr[z] = total(gyr, ny)
        start_all(gzr, z, nz, to_z, gzss, gzsr)
        for d in [e for e in (1, 3, 2) if e < ny]:
            yy = lax.rem(y + d, ny)
            for zz in range(nz):
                copy(img.at[yy, zz], img.at[yy, zz], iys.at[d, 0], iyr.at[yy, zz], to_y(yy)).wait_recv()
            qacc[...] += project(yy)

        for h in range(nc):
            qds[h] = qacc[:, h * half : (h + 1) * half]
        qd = copy(qds.at[other], qdr, qdsem.at[0], qdsem.at[1], to_core())
        qd.start()
        wait_all(gzr, z, nz, to_z, gzss, gzsr)
        gall[j] = total(gzr, nz)
        start_all(gall, j, nxc, to_j, gass, gasr)
        qd.wait_recv()
        qxr[x] = (qds[c] + qdr[...]).astype(BF16)
        start_all(qxr, x, nx, to_x, qxss, qxsr)
        wait_all(gall, j, nxc, to_j, gass, gasr)
        gc = gall[...].reshape(k, 2 * k)
        inv = inverse(gc[:, :k])
        back = nn_fine(gc[:, k:], inv)
        ginv[...] = inv
        xt[...] += nn_fine(back, pt[...])
        wait_all(qxr, x, nx, to_x, qxss, qxsr)
        qf[c] = total(qxr, nx)
        qfc = copy(qf.at[c], qf.at[c], qfsem.at[0], qfsem.at[1], to_core())
        qfc.start()
        copy(qf.at[other], qf.at[other], qfsem.at[0], qfsem.at[1], to_core()).wait_recv()
        qt[...] = jnp.concatenate([qf[h] for h in range(nc)], 1) + pt[...]
        rt[...] -= nn_fine(back, qt[...])

        @pl.when(step + 1 < iters)
        def _():
            @pl.when(x < nblk)
            def _():
                plane_start(own_block(qt[...]))

            @pl.when(x == nblk)
            def _():
                cross = nt_fine(rt[...], qt[...])
                plane_start(jnp.concatenate([cross, jnp.zeros((k, LANES - k), F32)], 1))

            plane_finish()
            image = gathered()
            proj = yt[...] - nn_fine(back, image)
            yt[...] = proj
            scaled = proj * shrink[...]
            cross = wall[nx - 1].astype(F32)[:, :k] + nt_fine(scaled, image)
            coef = nn_fine(cross, ginv[...])
            pt[...] = rt[...] + spread(scaled) - nn_fine(coef, pt[...])

        for p, off in enumerate(pair_order):
            for d in range(1, ny):
                s1_copy(d, p).wait_send()
            for b in range(2 if off else 1):
                s2_copy(p, b, mate).wait_send()
        for d in range(1, nz):
            copy(img.at[y, z], img.at[y, z], izs.at[d], izr.at[z], to_z(mate)).wait_send()
        for e in range(1, ny):
            for d in range(nz):
                iy_copy(e, z, d).wait_send()
        for d in range(1, nxc):
            jj = lax.rem(j + d, nxc)
            copy(gxs.at[jj], gxr.at[j], gxss.at[d], gxsr.at[j], to_j(jj)).wait_send()
        sent_all(gyr, y, ny, to_y, gyss, gysr)
        sent_all(gzr, z, nz, to_z, gzss, gzsr)
        sent_all(gall, j, nxc, to_j, gass, gasr)
        qd.wait_send()
        sent_all(qxr, x, nx, to_x, qxss, qxsr)
        qfc.wait_send()
        return carry

    lax.fori_loop(0, iters, iteration, 0)
    mine_rows = pl.ds(pl.multiple_of(c * (k // nc), k // nc), k // nc)
    x_out[...] = xt[mine_rows, :]
    r_out[...] = rt[mine_rows, :]


def shards(sizes, design, right_side, factor, nystrom_values):
    nx, nf, nc, ny = sizes
    nz = nf // ny
    nxc, npair = nx * nc, nz // 2
    samples, feats = design.shape
    k = right_side.shape[1] * nc
    rank_half = factor.shape[1]
    shrink = (1.0 + jnp.min(nystrom_values)) / (1.0 + nystrom_values) - 1.0
    vmem = pl.BlockSpec(memory_space=pltpu.VMEM)
    dma = pltpu.SemaphoreType.DMA
    piece = (k // nxc, 2 * k)
    half = feats // nc
    scratch = [
        pltpu.VMEM((samples, feats), BF16),
        pltpu.VMEM((nc, k // nc, feats), F32),
        pltpu.VMEM((nc, feats, rank_half), BF16),
        pltpu.VMEM((k, feats), F32),
        pltpu.VMEM((k, feats), F32),
        pltpu.VMEM((k, feats), F32),
        pltpu.VMEM((k, nc * rank_half), F32),
        pltpu.VMEM((k, k), F32),
        pltpu.VMEM((k, feats), F32),
        pltpu.VMEM((ny - 1, npair, k, 2 * LANES), BF16),
        pltpu.VMEM((ny - 1, npair, k, 2 * LANES), BF16),
        pltpu.VMEM((npair, k, 2 * LANES), F32),
        pltpu.VMEM((npair, 2, k, LANES), BF16),
        pltpu.VMEM((nz, k, LANES), BF16),
        pltpu.VMEM((2, k, LANES), F32),
        pltpu.VMEM((ny, nz, k, LANES), BF16),
        pltpu.VMEM((k, feats), F32),
        pltpu.VMEM((nxc, *piece), F32),
        pltpu.VMEM((nxc, *piece), F32),
        pltpu.VMEM((ny, *piece), F32),
        pltpu.VMEM((nz, *piece), F32),
        pltpu.VMEM((nxc, *piece), F32),
        pltpu.VMEM((nc, k, half), F32),
        pltpu.VMEM((k, half), F32),
        pltpu.VMEM((nx, k, half), BF16),
        pltpu.VMEM((nc, k, half), F32),
        pltpu.VMEM((ny, k, LANES), WIRE),
        pltpu.VMEM((nz, k, LANES), WIRE),
        pltpu.VMEM((nxc, k, LANES), WIRE),
        dma((ny,)), dma((2,)), dma((2,)),
        dma((ny - 1, npair)), dma((ny - 1, npair)), dma((npair, 2)), dma((nz,)),
        dma((nz,)), dma((nz,)), dma((ny, nz)), dma((ny, nz)),
        dma((nxc,)), dma((nxc,)), dma((ny,)), dma((ny,)), dma((nz,)), dma((nz,)), dma((nxc,)), dma((nxc,)),
        dma((2,)), dma((nx,)), dma((nx,)), dma((2,)),
        dma((ny,)), dma((ny,)), dma((nz,)), dma((nz,)), dma((nxc,)), dma((nxc,)),
    ]
    shape = jax.ShapeDtypeStruct((k // nc, feats), F32)
    sol, res = pl.pallas_call(
        functools.partial(kernel, (nx, nc, nz, ny, ITERS)),
        out_shape=(shape, shape),
        in_specs=[pl.BlockSpec(memory_space=pl.ANY), vmem, vmem, vmem],
        out_specs=(vmem, vmem),
        scratch_shapes=scratch,
        compiler_params=pltpu.CompilerParams(
            collective_id=0, has_side_effects=True, vmem_limit_bytes=56 * 2**20
        ),
        name="solve",
    )(design, right_side.T, factor, shrink[None, :])
    return sol.T, res.T


def solution(mesh):
    placed = (P(("samples", "rhs"), "features"), P("features", "rhs"), P("features", "rhs"), P())
    nx, nf, nc = (mesh.shape[a] for a in ("samples", "features", "rhs"))
    ny = max(2, nf // 8)
    return jax.shard_map(
        functools.partial(shards, (nx, nf, nc, ny)),
        mesh=mesh,
        in_specs=placed,
        out_specs=(P("features", "rhs"), P("features", "rhs")),
        check_vma=False,
    )
```

time: 721 us -> 187 us (0.26); the launches traced: 706 us -> 187 us
  waiting for transfers between devices: 298 us -> 0 us
  starting transfers between devices: 191 us -> 0 us
  Pallas kernels: 0 us -> 180 us
  blocking collectives: 60.5 us -> 0 us
  other arithmetic: 62.4 us -> 1.99 us
  matrix products: 53 us -> 0 us
  local copies, waits for them, and re-layouts: 38.2 us -> 3.72 us
    all_to_all x34 -> x0, waiting for transfers between devices: 298 us -> none  [the longest x20 167 us: sent_to_all(): lax.all_to_all(jnp.broadcast_to(array[None], (size, *array.shape)), axis,...]
    all_to_all x34 -> x0, starting transfers between devices: 191 us -> none  [the longest x20 125 us: sent_to_all(): lax.all_to_all(jnp.broadcast_to(array[None], (size, *array.shape)), axis,...]
    pallas_call x0 -> x1, Pallas kernels: none -> 180 us  [shards(): pl.pallas_call(functools.partial(kernel, (nx, nc, nz, ny, ITERS)), out_sh...]
    all_to_all x3 -> x0, blocking collectives: 60.5 us -> none  [the longest x2 41.2 us: summed_on_arrival(): lax.all_to_all(parts, axis, split_axis=0, concat_axis=0, tiled=True)]
    dot_general x42 -> x0, matrix products: 49 us -> none  [the longest x3 18.1 us: shards(): jnp.dot(design, narrow, preferred_element_type=jnp.float32)]
    another operation x15 -> x0, other arithmetic: 36.2 us -> none  [the longest x9 19.6 us: shards(): chol_lower = jnp.linalg.cholesky(gram_block)]
    unnamed x71 -> x2, local copies, waits for them, and re-layouts: 23.9 us -> 3.14 us
    all_to_all x26 -> x0, other arithmetic: 20 us -> none  [the longest x13 10 us: sent_to_all(): lax.all_to_all(jnp.broadcast_to(array[None], (size, *array.shape)), axis,...]
  transfers between devices with their start and end apart: 34 -> 0, of which waited for: 32 -> 0; matrix products, arithmetic and copies ran while one was open for 11% -> 0% of each run, Pallas kernels for 0% -> 0%
where the time goes in v1:
time: 187 us
  Pallas kernels  180 us (96%)
  local copies, waits for them, and re-layouts  3.72 us (2%)
  other arithmetic  1.99 us (1%)
    pallas_call x1, Pallas kernels, shards(): pl.pallas_call(functools.partial(kernel, (nx, nc, nz, ny, ITERS)), out_sh...  180 us

profile of v1, /device:TPU:1, one launch (start us, length us, event | category | flops | bytes accessed | tf_op | source)
XLA Modules:
  0.0 187.2 jit_solution(11288934976966967961)
XLA Ops:
  0.6 1.3 reduce_min.9
  2.6 0.7 divide_add_fusion
  3.3 0.6 broadcast_in_dim.3.shrink
  3.9 180.2 %solve.1 = (f32[32,1024]{1,0:T(8,128)}, f32[32,1024]{1,0:T(8,128)}) custom-call(bf16[4096,1024]{1,0:T(8,128)(2,1)} %d_hbm.1, f32[32,1024]{1,0:T(8,128)} %bitcast.3, bf16[1024,384]{1,0:T(8,128)(2,1)} %f_in.1, f32[1,768]{1,0:T(1,128)} %broadcast_in_dim.3.shrink), custom_call_target="tpu_custom_call" | custom-call | tf_op jit(solution)/shard_map/solve/pallas_call | solution.py:418
  184.1 1.6 copy.8
  185.6 1.6 copy.9

commit v2 on v1

--- a/solution.py
+++ b/solution.py
@@ -12,7 +12,6 @@
 MESH = pl.DeviceIdType.MESH
 F32 = jnp.float32
 BF16 = jnp.bfloat16
-WIRE = jnp.float32
 
 
 def nt(a, b):
@@ -51,24 +50,34 @@
     n = a.shape[0]
     lane = lax.broadcasted_iota(jnp.int32, (1, n), 1)
     sub = lax.broadcasted_iota(jnp.int32, (n, 1), 0)
-    for i in range(n):
-        pivot = 1.0 / a[i : i + 1, i : i + 1]
-        row = jnp.where(lane == i, 1.0, a[i : i + 1, :]) * pivot
-        col = a[:, i : i + 1]
-        rest = jnp.where(lane == i, 0.0, a) - col * row
-        a = jnp.where(sub == i, row, rest)
-    return a
+    diagonal = jnp.where(lane == sub, a, 0.0)
+    scale_row = lax.rsqrt(jnp.sum(diagonal, axis=0, keepdims=True))
+    scale_col = lax.rsqrt(jnp.sum(diagonal, axis=1, keepdims=True))
+    a = a * scale_row * scale_col
+    for i in range(0, n, 2):
+        r1, r2 = a[i : i + 1, :], a[i + 1 : i + 2, :]
+        c1, c2 = a[:, i : i + 1], a[:, i + 1 : i + 2]
+        p, q = a[i : i + 1, i : i + 1], a[i : i + 1, i + 1 : i + 2]
+        t, s = a[i + 1 : i + 2, i : i + 1], a[i + 1 : i + 2, i + 1 : i + 2]
+        over = 1.0 / (p * s - q * t)
+        e1 = jnp.where(lane == i, 1.0, jnp.where(lane == i + 1, 0.0, r1))
+        e2 = jnp.where(lane == i + 1, 1.0, jnp.where(lane == i, 0.0, r2))
+        u1 = (s * e1 - q * e2) * over
+        u2 = (p * e2 - t * e1) * over
+        rest = jnp.where((lane == i) | (lane == i + 1), 0.0, a) - c1 * u1 - c2 * u2
+        a = jnp.where(sub == i, u1, jnp.where(sub == i + 1, u2, rest))
+    return a * scale_row * scale_col
 
 
 def kernel(
     dims,
-    d_hbm, rt_in, f_in, shrink,
-    x_out, r_out,
+    d_hbm, rt_in, f_in, values,
+    out,
     dv, rfull, fall, pt, rt, xt, yt, ginv, qt,
     s1, r1, acc1, s2, r2, own2, img, qacc,
     gxs, gxr, gyr, gzr, gall,
     qds, qdr, qxr, qf,
-    wyr, wzr, wall,
+    wys, wyr, wzr, wall, back, shrink,
     dsem, rsem, fsem,
     s1s, s1r, s2s, s2r, izs, izr, iys, iyr,
     gxss, gxsr, gyss, gysr, gzss, gzsr, gass, gasr,
@@ -77,6 +86,8 @@
 ):
     nx, nc, nz, ny, iters = dims
     nxc, npair, nblk = nx * nc, nz // 2, nx - 1
+    near = [(dy, dx, dc) for dy in range(ny) for dx in range(nx) for dc in range(nc) if dy + dx + dc]
+    near.sort(key=lambda o: -(min(o[0], ny - o[0]) + min(o[1], nx - o[1]) + 0.1 * o[2]))
     k = pt.shape[0]
     feats = pt.shape[1]
     half = feats // nc
@@ -102,6 +113,13 @@
     def to_j(jj):
         return {"samples": lax.rem(jj, nx), "rhs": lax.div(jj, nx)}
 
+    def moved(offset):
+        dy, dx, dc = offset
+        return lax.rem(y + dy, ny), lax.rem(x + dx, nx), lax.rem(c + dc, nc)
+
+    def to_near(yy, xx, cc):
+        return {"samples": xx, "features": z * ny + yy, "rhs": cc}
+
     def copy(src, dst, ss, rs, dev):
         return pltpu.make_async_remote_copy(
             src_ref=src, dst_ref=dst, send_sem=ss, recv_sem=rs, device_id=dev, device_id_type=MESH
@@ -136,13 +154,11 @@
         load.start()
 
     barrier = pltpu.get_barrier_semaphore()
-    for d in range(1, ny):
-        pl.semaphore_signal(barrier, inc=1, device_id=to_y(lax.rem(y + d, ny)), device_id_type=MESH)
     for d in range(1, nz):
         pl.semaphore_signal(barrier, inc=1, device_id=to_z(lax.rem(z + d, nz)), device_id_type=MESH)
-    for d in range(1, nxc):
-        pl.semaphore_signal(barrier, inc=1, device_id=to_j(lax.rem(j + d, nxc)), device_id_type=MESH)
-    pl.semaphore_wait(barrier, ny + nz + nxc - 3)
+    for offset in near:
+        pl.semaphore_signal(barrier, inc=1, device_id=to_near(*moved(offset)), device_id_type=MESH)
+    pl.semaphore_wait(barrier, nz - 1 + len(near))
 
     send_r = copy(rt_in, rfull.at[c], rsem.at[0], rsem.at[1], to_core())
     send_r.start()
@@ -151,24 +167,47 @@
     rfull[c] = rt_in[...]
     fall[c] = f_in[...]
 
-    def plane_start(value):
-        wyr[y] = value.astype(WIRE)
-        start_all(wyr, y, ny, to_y, wyss, wysr)
+    quarter = k // ny
+
+    def plane_sum(value):
+        wys[...] = value.reshape(wys.shape)
+        for d in range(1, ny):
+            yy = lax.rem(y + d, ny)
+            copy(wys.at[yy], wyr.at[y], wyss.at[d], wysr.at[y], to_y(yy)).start()
+        wyr[y] = wys[y]
+
+    def plane_exchange():
+        wait_all(wyr, y, ny, to_y, wyss, wysr)
+        wzr[z] = total(wyr, ny)
+        start_all(wzr, z, nz, to_z, wzss, wzsr)
+
+    def near_copy(n, offset, source):
+        yy, xx, cc = moved(offset)
+        if source:
+            return copy(wall.at[cc * nx + xx, yy], wall.at[cc * nx + xx, yy], wxss.at[n], wxsr.at[cc * nx + xx, yy], to_near(yy, xx, cc))
+        return copy(wall.at[j, y], wall.at[j, y], wxss.at[n], wxsr.at[j, y], to_near(yy, xx, cc))
 
     def plane_finish():
-        wait_all(wyr, y, ny, to_y, wyss, wysr)
-        wzr[z] = total(wyr, ny).astype(WIRE)
-        start_all(wzr, z, nz, to_z, wzss, wzsr)
-        sent_all(wyr, y, ny, to_y, wyss, wysr)
         wait_all(wzr, z, nz, to_z, wzss, wzsr)
-        wall[j] = total(wzr, nz).astype(WIRE)
-        start_all(wall, j, nxc, to_j, wxss, wxsr)
+        whole = total(wzr, nz)
+        upper, lower = halves(whole)
+        wall[j, y] = jnp.where((x == nblk) & (c == 1), lower.astype(F32), upper.astype(F32)).astype(BF16)
+        for n, offset in enumerate(near):
+            near_copy(n, offset, False).start()
+        for n, offset in enumerate(near):
+            near_copy(n, offset, True).wait_recv()
+        for d in range(1, ny):
+            yy = lax.rem(y + d, ny)
+            copy(wys.at[yy], wyr.at[y], wyss.at[d], wysr.at[y], to_y(yy)).wait_send()
         sent_all(wzr, z, nz, to_z, wzss, wzsr)
-        wait_all(wall, j, nxc, to_j, wxss, wxsr)
-        sent_all(wall, j, nxc, to_j, wxss, wxsr)
+        for n, offset in enumerate(near):
+            near_copy(n, offset, False).wait_send()
+
+    def block(jj):
+        return wall[jj].astype(F32).reshape(k, LANES)
 
     def gathered():
-        return jnp.concatenate([wall[cc * nx + b].astype(F32) for cc in range(nc) for b in range(nblk)], 1)
+        return jnp.concatenate([block(cc * nx + b) for cc in range(nc) for b in range(nblk)], 1)
 
     def own_block(value):
         return rows_fine(value, nn, f_in[:, pl.ds(pl.multiple_of(x * LANES, LANES), LANES)])
@@ -177,18 +216,20 @@
         out = rows_fine(scaled[:, :rank_half], nt, fall[0])
         return out + rows_fine(scaled[:, rank_half:], nt, fall[1])
 
+    shrink[...] = (1.0 + jnp.min(values[...], axis=1, keepdims=True)) / (1.0 + values[...]) - 1.0
     copy(rt_in, rfull.at[other], rsem.at[0], rsem.at[1], to_core()).wait_recv()
     rt[...] = rfull[...].reshape(k, feats)
     xt[...] = jnp.zeros_like(xt)
 
     @pl.when(x < nblk)
     def _():
-        plane_start(own_block(rt[...]))
+        plane_sum(own_block(rt[...]))
 
     @pl.when(x == nblk)
     def _():
-        plane_start(jnp.zeros((k, LANES), F32))
-
+        plane_sum(jnp.zeros((k, LANES), F32))
+
+    plane_exchange()
     plane_finish()
     copy(f_in, fall.at[other], fsem.at[0], fsem.at[1], to_core()).wait_recv()
     send_r.wait_send()
@@ -221,14 +262,20 @@
         narrow = pt[...].astype(BF16)
         for p, off in enumerate(pair_order):
             q = lax.rem(zq + off, npair)
-            for d in [*y_order, 0]:
-                base = lax.rem(y + d, ny) * rows + q * (2 * LANES)
-                part = nt(narrow, dv[pl.ds(pl.multiple_of(base, 2 * LANES), 2 * LANES), :])
-                if d:
-                    s1[d - 1, p] = part.astype(BF16)
-                    s1_copy(d, p).start()
-                else:
-                    acc1[p] = part
+            order = [*y_order, 0]
+            for n in range(0, len(order), 2):
+                parts = []
+                for d in order[n : n + 2]:
+                    base = lax.rem(y + d, ny) * rows + q * (2 * LANES)
+                    parts.append(nt(narrow, dv[pl.ds(pl.multiple_of(base, 2 * LANES), 2 * LANES), :]))
+                for d, part in zip(order[n : n + 2], parts):
+                    if d:
+                        s1[d - 1, p] = part.astype(BF16)
+                    else:
+                        acc1[p] = part
+                for d in order[n : n + 2]:
+                    if d:
+                        s1_copy(d, p).start()
         for p, off in enumerate(pair_order):
             tot = acc1[p]
             for d in range(1, ny):
@@ -298,43 +345,56 @@
             qds[h] = qacc[:, h * half : (h + 1) * half]
         qd = copy(qds.at[other], qdr, qdsem.at[0], qdsem.at[1], to_core())
         qd.start()
+        qd.wait_recv()
+        qxr[x] = (qds[c] + qdr[...]).astype(BF16)
+        start_all(qxr, x, nx, to_x, qxss, qxsr)
         wait_all(gzr, z, nz, to_z, gzss, gzsr)
         gall[j] = total(gzr, nz)
         start_all(gall, j, nxc, to_j, gass, gasr)
-        qd.wait_recv()
-        qxr[x] = (qds[c] + qdr[...]).astype(BF16)
-        start_all(qxr, x, nx, to_x, qxss, qxsr)
-        wait_all(gall, j, nxc, to_j, gass, gasr)
-        gc = gall[...].reshape(k, 2 * k)
-        inv = inverse(gc[:, :k])
-        back = nn_fine(gc[:, k:], inv)
-        ginv[...] = inv
-        xt[...] += nn_fine(back, pt[...])
+
+        def step_coefficient():
+            wait_all(gall, j, nxc, to_j, gass, gasr)
+            gc = gall[...].reshape(k, 2 * k)
+            inv = inverse(gc[:, :k])
+            ginv[...] = inv
+            back[...] = nn_fine(gc[:, k:], inv)
+            xt[...] += nn_fine(back[...], pt[...])
+
+        @pl.when(step + 1 == iters)
+        def _():
+            step_coefficient()
+
         wait_all(qxr, x, nx, to_x, qxss, qxsr)
         qf[c] = total(qxr, nx)
         qfc = copy(qf.at[c], qf.at[c], qfsem.at[0], qfsem.at[1], to_core())
         qfc.start()
         copy(qf.at[other], qf.at[other], qfsem.at[0], qfsem.at[1], to_core()).wait_recv()
         qt[...] = jnp.concatenate([qf[h] for h in range(nc)], 1) + pt[...]
-        rt[...] -= nn_fine(back, qt[...])
+
+        @pl.when(step + 1 == iters)
+        def _():
+            rt[...] -= nn_fine(back[...], qt[...])
 
         @pl.when(step + 1 < iters)
         def _():
             @pl.when(x < nblk)
             def _():
-                plane_start(own_block(qt[...]))
+                plane_sum(own_block(qt[...]))
 
             @pl.when(x == nblk)
             def _():
-                cross = nt_fine(rt[...], qt[...])
-                plane_start(jnp.concatenate([cross, jnp.zeros((k, LANES - k), F32)], 1))
-
+                plane_sum(jnp.concatenate([nt_fine(rt[...], qt[...]), nt_fine(qt[...], qt[...])], 1))
+
+            plane_exchange()
+            step_coefficient()
+            rt[...] -= nn_fine(back[...], qt[...])
             plane_finish()
             image = gathered()
-            proj = yt[...] - nn_fine(back, image)
+            small = block(nx - 1) + block(nx * nc - 1)
+            proj = yt[...] - nn_fine(back[...], image)
             yt[...] = proj
             scaled = proj * shrink[...]
-            cross = wall[nx - 1].astype(F32)[:, :k] + nt_fine(scaled, image)
+            cross = small[:, :k] - nn_fine(back[...], small[:, k:]) + nt_fine(scaled, image)
             coef = nn_fine(cross, ginv[...])
             pt[...] = rt[...] + spread(scaled) - nn_fine(coef, pt[...])
 
@@ -361,8 +421,8 @@
 
     lax.fori_loop(0, iters, iteration, 0)
     mine_rows = pl.ds(pl.multiple_of(c * (k // nc), k // nc), k // nc)
-    x_out[...] = xt[mine_rows, :]
-    r_out[...] = rt[mine_rows, :]
+    out[0] = xt[mine_rows, :]
+    out[1] = rt[mine_rows, :]
 
 
 def shards(sizes, design, right_side, factor, nystrom_values):
@@ -372,7 +432,6 @@
     samples, feats = design.shape
     k = right_side.shape[1] * nc
     rank_half = factor.shape[1]
-    shrink = (1.0 + jnp.min(nystrom_values)) / (1.0 + nystrom_values) - 1.0
     vmem = pl.BlockSpec(memory_space=pltpu.VMEM)
     dma = pltpu.SemaphoreType.DMA
     piece = (k // nxc, 2 * k)
@@ -404,29 +463,31 @@
         pltpu.VMEM((k, half), F32),
         pltpu.VMEM((nx, k, half), BF16),
         pltpu.VMEM((nc, k, half), F32),
-        pltpu.VMEM((ny, k, LANES), WIRE),
-        pltpu.VMEM((nz, k, LANES), WIRE),
-        pltpu.VMEM((nxc, k, LANES), WIRE),
+        pltpu.VMEM((ny, k // ny, LANES), F32),
+        pltpu.VMEM((ny, k // ny, LANES), F32),
+        pltpu.VMEM((nz, k // ny, LANES), F32),
+        pltpu.VMEM((nxc, ny, k // ny, LANES), BF16),
+        pltpu.VMEM((k, k), F32),
+        pltpu.VMEM((1, nc * rank_half), F32),
         dma((ny,)), dma((2,)), dma((2,)),
         dma((ny - 1, npair)), dma((ny - 1, npair)), dma((npair, 2)), dma((nz,)),
         dma((nz,)), dma((nz,)), dma((ny, nz)), dma((ny, nz)),
         dma((nxc,)), dma((nxc,)), dma((ny,)), dma((ny,)), dma((nz,)), dma((nz,)), dma((nxc,)), dma((nxc,)),
         dma((2,)), dma((nx,)), dma((nx,)), dma((2,)),
-        dma((ny,)), dma((ny,)), dma((nz,)), dma((nz,)), dma((nxc,)), dma((nxc,)),
+        dma((ny,)), dma((ny,)), dma((nz,)), dma((nz,)), dma((nxc * ny,)), dma((nxc, ny)),
     ]
-    shape = jax.ShapeDtypeStruct((k // nc, feats), F32)
-    sol, res = pl.pallas_call(
+    out = pl.pallas_call(
         functools.partial(kernel, (nx, nc, nz, ny, ITERS)),
-        out_shape=(shape, shape),
+        out_shape=jax.ShapeDtypeStruct((2, k // nc, feats), F32),
         in_specs=[pl.BlockSpec(memory_space=pl.ANY), vmem, vmem, vmem],
-        out_specs=(vmem, vmem),
+        out_specs=vmem,
         scratch_shapes=scratch,
         compiler_params=pltpu.CompilerParams(
             collective_id=0, has_side_effects=True, vmem_limit_bytes=56 * 2**20
         ),
         name="solve",
-    )(design, right_side.T, factor, shrink[None, :])
-    return sol.T, res.T
+    )(design, right_side.T, factor, nystrom_values[None, :])
+    return out[0].T, out[1].T
 
 
 def solution(mesh):

time: 187 us -> 166 us (0.89)
  Pallas kernels: 180 us -> 163 us
  other arithmetic: 1.99 us -> 0 us
    pallas_call x1, Pallas kernels: 180 us -> 163 us  [shards(): pl.pallas_call(functools.partial(kernel, (nx, nc, nz, ny, ITERS)), out_sh...]
    unnamed x2 -> x0, local copies, waits for them, and re-layouts: 3.14 us -> none
where the time goes in v2:
time: 166 us
  Pallas kernels  163 us (98%)
  local copies, waits for them, and re-layouts  2.95 us (2%)
    pallas_call x1, Pallas kernels, shards(): pl.pallas_call(functools.partial(kernel, (nx, nc, nz, ny, ITERS)), out_sh...  163 us

profile of v2, /device:TPU:1, one launch (start us, length us, event | category | flops | bytes accessed | tf_op | source)
XLA Modules:
  0.0 166.3 jit_solution(16380090424043269478)
XLA Ops:
  0.6 1.3 broadcast_in_dim.3.values
  1.9 162.7 %solve.1 = f32[2,32,1024]{2,1,0:T(8,128)} custom-call(bf16[4096,1024]{1,0:T(8,128)(2,1)} %d_hbm.1, f32[32,1024]{1,0:T(8,128)} %bitcast.9, bf16[1024,384]{1,0:T(8,128)(2,1)} %f_in.1, f32[1,768]{1,0:T(1,128)} %broadcast_in_dim.3.values), custom_call_target="tpu_custom_call" | custom-call | tf_op jit(solution)/shard_map/solve/pallas_call | solution.py:479
  164.6 1.7 %slice_bitcast_fusion = (f32[1024,32]{0,1:T(8,128)}, f32[1024,32]{0,1:T(8,128)}) fusion(f32[2,32,1024]{2,1,0:T(8,128)} %solve.1), kind=kLoop, calls=%fused_computation | loop fusion | bytes 524288 | tf_op jit(solution)/shard_map/transpose | solution.py:490

commit v3 on v2

--- a/solution.py
+++ b/solution.py
@@ -28,10 +28,17 @@
     return upper, lower
 
 
+def wide(a):
+    upper, lower = halves(a)
+    return jnp.concatenate([upper, upper, lower, lower], 1)
+
+
+def tall(b):
+    return jnp.concatenate(halves(b) * 2, 0)
+
+
 def nn_fine(a, b):
-    ah, al = halves(a)
-    bh, bl = halves(b)
-    return nn(jnp.concatenate([ah, ah, al, al], 1), jnp.concatenate([bh, bl, bh, bl], 0))
+    return nn(wide(a), tall(b))
 
 
 def nt_fine(a, b):
@@ -46,46 +53,51 @@
     return t[:m] + t[m:]
 
 
-def inverse(a):
+def inverse(a, width=8):
     n = a.shape[0]
     lane = lax.broadcasted_iota(jnp.int32, (1, n), 1)
     sub = lax.broadcasted_iota(jnp.int32, (n, 1), 0)
-    diagonal = jnp.where(lane == sub, a, 0.0)
-    scale_row = lax.rsqrt(jnp.sum(diagonal, axis=0, keepdims=True))
-    scale_col = lax.rsqrt(jnp.sum(diagonal, axis=1, keepdims=True))
-    a = a * scale_row * scale_col
-    for i in range(0, n, 2):
-        r1, r2 = a[i : i + 1, :], a[i + 1 : i + 2, :]
-        c1, c2 = a[:, i : i + 1], a[:, i + 1 : i + 2]
-        p, q = a[i : i + 1, i : i + 1], a[i : i + 1, i + 1 : i + 2]
-        t, s = a[i + 1 : i + 2, i : i + 1], a[i + 1 : i + 2, i + 1 : i + 2]
-        over = 1.0 / (p * s - q * t)
-        e1 = jnp.where(lane == i, 1.0, jnp.where(lane == i + 1, 0.0, r1))
-        e2 = jnp.where(lane == i + 1, 1.0, jnp.where(lane == i, 0.0, r2))
-        u1 = (s * e1 - q * e2) * over
-        u2 = (p * e2 - t * e1) * over
-        rest = jnp.where((lane == i) | (lane == i + 1), 0.0, a) - c1 * u1 - c2 * u2
-        a = jnp.where(sub == i, u1, jnp.where(sub == i + 1, u2, rest))
-    return a * scale_row * scale_col
+    for i in range(0, n, width):
+        cols = [jnp.broadcast_to(a[:, i + t : i + t + 1], (n, n)) for t in range(width)]
+        pivots = [[cols[t][i + r : i + r + 1, :] for t in range(width)] for r in range(width)]
+        inside = (lane >= i) & (lane < i + width)
+        rows = [jnp.where(lane == i + r, 1.0, jnp.where(inside, 0.0, a[i + r : i + r + 1, :])) for r in range(width)]
+        for r in range(width):
+            over = 1.0 / pivots[r][r]
+            rows[r] = rows[r] * over
+            for t in range(r + 1, width):
+                pivots[r][t] = pivots[r][t] * over
+            for q in range(width):
+                if q != r:
+                    factor = pivots[q][r]
+                    rows[q] = rows[q] - factor * rows[r]
+                    for t in range(r + 1, width):
+                        pivots[q][t] = pivots[q][t] - factor * pivots[r][t]
+        a = jnp.where(inside, 0.0, a)
+        for r in range(width):
+            a = a - cols[r] * rows[r]
+        for r in range(width):
+            a = jnp.where(sub == i + r, rows[r], a)
+    return a
 
 
 def kernel(
     dims,
     d_hbm, rt_in, f_in, values,
     out,
-    dv, rfull, fall, pt, rt, xt, yt, ginv, qt,
-    s1, r1, acc1, s2, r2, own2, img, qacc,
+    dv, rfull, fall, pt, rt, xt, yt, gp, qt,
+    s0, r0, s1, r1, acc0, acc1, s2, r2, img, qacc,
     gxs, gxr, gyr, gzr, gall,
     qds, qdr, qxr, qf,
     wys, wyr, wzr, wall, back, shrink,
     dsem, rsem, fsem,
-    s1s, s1r, s2s, s2r, izs, izr, iys, iyr,
+    s0s, s0r, s1s, s1r, s2s, s2r, izs, izr, iys, iyr, ifs,
     gxss, gxsr, gyss, gysr, gzss, gzsr, gass, gasr,
     qdsem, qxss, qxsr, qfsem,
     wyss, wysr, wzss, wzsr, wxss, wxsr,
 ):
     nx, nc, nz, ny, iters = dims
-    nxc, npair, nblk = nx * nc, nz // 2, nx - 1
+    nxc, nblk = nx * nc, nx - 1
     near = [(dy, dx, dc) for dy in range(ny) for dx in range(nx) for dc in range(nc) if dy + dx + dc]
     near.sort(key=lambda o: -(min(o[0], ny - o[0]) + min(o[1], nx - o[1]) + 0.1 * o[2]))
     k = pt.shape[0]
@@ -150,6 +162,10 @@
         pltpu.make_async_copy(d_hbm.at[pl.ds(i * rows, rows)], dv.at[pl.ds(i * rows, rows)], dsem.at[i])
         for i in range(ny)
     ]
+    load_r = pltpu.make_async_copy(rt_in, rfull.at[c], dsem.at[ny])
+    load_f = pltpu.make_async_copy(f_in, fall.at[c], dsem.at[ny + 1])
+    load_r.start()
+    load_f.start()
     for load in loads:
         load.start()
 
@@ -160,12 +176,12 @@
         pl.semaphore_signal(barrier, inc=1, device_id=to_near(*moved(offset)), device_id_type=MESH)
     pl.semaphore_wait(barrier, nz - 1 + len(near))
 
-    send_r = copy(rt_in, rfull.at[c], rsem.at[0], rsem.at[1], to_core())
+    load_r.wait()
+    send_r = copy(rfull.at[c], rfull.at[c], rsem.at[0], rsem.at[1], to_core())
     send_r.start()
-    send_f = copy(f_in, fall.at[c], fsem.at[0], fsem.at[1], to_core())
+    load_f.wait()
+    send_f = copy(fall.at[c], fall.at[c], fsem.at[0], fsem.at[1], to_core())
     send_f.start()
-    rfull[c] = rt_in[...]
-    fall[c] = f_in[...]
 
     quarter = k // ny
 
@@ -204,20 +220,23 @@
             near_copy(n, offset, False).wait_send()
 
     def block(jj):
-        return wall[jj].astype(F32).reshape(k, LANES)
+        return wall[jj].reshape(k, LANES)
 
     def gathered():
         return jnp.concatenate([block(cc * nx + b) for cc in range(nc) for b in range(nblk)], 1)
 
     def own_block(value):
-        return rows_fine(value, nn, f_in[:, pl.ds(pl.multiple_of(x * LANES, LANES), LANES)])
+        return rows_fine(value, nn, fall[c, :, pl.ds(pl.multiple_of(x * LANES, LANES), LANES)])
 
     def spread(scaled):
         out = rows_fine(scaled[:, :rank_half], nt, fall[0])
         return out + rows_fine(scaled[:, rank_half:], nt, fall[1])
 
-    shrink[...] = (1.0 + jnp.min(values[...], axis=1, keepdims=True)) / (1.0 + values[...]) - 1.0
-    copy(rt_in, rfull.at[other], rsem.at[0], rsem.at[1], to_core()).wait_recv()
+    least = jnp.min(jnp.min(values[...], axis=1, keepdims=True), axis=0, keepdims=True)
+    table = (1.0 + least) / (1.0 + values[...]) - 1.0
+    for r in range(values.shape[0]):
+        shrink[:, r * LANES : (r + 1) * LANES] = table[r : r + 1, :]
+    copy(rfull.at[c], rfull.at[other], rsem.at[0], rsem.at[1], to_core()).wait_recv()
     rt[...] = rfull[...].reshape(k, feats)
     xt[...] = jnp.zeros_like(xt)
 
@@ -231,78 +250,122 @@
 
     plane_exchange()
     plane_finish()
-    copy(f_in, fall.at[other], fsem.at[0], fsem.at[1], to_core()).wait_recv()
+    copy(fall.at[c], fall.at[other], fsem.at[0], fsem.at[1], to_core()).wait_recv()
     send_r.wait_send()
     send_f.wait_send()
-    yt[...] = gathered()
+    yt[...] = gathered().astype(F32)
     pt[...] = rt[...] + spread(yt[...] * shrink[...])
     for load in loads:
         load.wait()
 
     y_order = [d for d in (2, 1, 3) if d < ny]
-    z_order = [d for d in (1, 7, 2, 6, 3, 5, 4) if d < nz]
-    pair_order = [(npair // 2 + s) % npair for s in (0, 3, 1, 2)][:npair] if npair == 4 else list(range(1, npair)) + [0]
-    pair_order = [p for p in pair_order if p] + [0]
-    zq, zb = lax.div(z, 2), lax.rem(z, 2)
-    mate = z + 1 - 2 * zb
-
-    def s1_copy(d, p):
-        return copy(s1.at[d - 1, p], r1.at[ny - d - 1, p], s1s.at[d - 1, p], s1r.at[ny - d - 1, p], to_y(lax.rem(y + d, ny)))
-
-    def r1_copy(d, p):
-        return copy(s1.at[d - 1, p], r1.at[d - 1, p], s1s.at[d - 1, p], s1r.at[d - 1, p], to_y(lax.rem(y + d, ny)))
-
-    def s2_copy(slot, b, zz):
-        return copy(s2.at[slot, b], r2.at[z], s2s.at[slot, b], s2r.at[z], to_z(zz))
-
-    def iy_copy(d, zz, zslot):
-        return copy(img.at[y, zz], img.at[y, zz], iys.at[d, zslot], iyr.at[y, zz], to_y(lax.rem(y + d, ny)))
+    beside = (1, nz - 1)
+    distant = sorted(range(2, nz - 1), key=lambda d: -min(d, nz - d))
+    arriving = distant[::-1]
+    pieces = [*distant, 0]
+    pairs = [(n, pieces[n : n + 2]) for n in range(0, len(pieces), 2)]
+
+    def along_z(d):
+        return lax.rem(z + d, nz)
+
+    def along_y(d):
+        return lax.rem(y + d, ny)
+
+    def products(narrow, parts, offsets):
+        start = [pl.multiple_of(along_y(d) * rows + along_z(o) * LANES, LANES) for d in parts for o in offsets]
+        part = nt(narrow, jnp.concatenate([dv[pl.ds(at, LANES), :] for at in start], 0))
+        cut = [part[:, n * LANES : (n + 1) * LANES] for n in range(len(start))]
+        return [(d, cut[n * len(offsets) : (n + 1) * len(offsets)]) for n, d in enumerate(parts)]
+
+    def s0_copy(b, d):
+        return copy(s0.at[b, d], r0.at[b, d], s0s.at[b, d], s0r.at[b, d], to_z(along_z(beside[b])))
+
+    def s1_copy(d, n, count, received=False):
+        at = pl.ds(n, count)
+        back_slot = d - 1 if received else ny - d - 1
+        return copy(s1.at[d - 1, at], r1.at[back_slot, at], s1s.at[d - 1, n], s1r.at[back_slot, n], to_y(along_y(d)))
+
+    def s2_copy(n, d):
+        return copy(s2.at[n], r2.at[z], s2s.at[n], s2r.at[z], to_z(along_z(d)))
+
+    def iy_copy(d, zz, slot):
+        return copy(img.at[y, zz], img.at[y, zz], iys.at[d, slot], iyr.at[y, zz], to_y(along_y(d)))
+
+    def if_copy(b, d):
+        yy = along_y(d)
+        return copy(img.at[yy, z], img.at[yy, z], ifs.at[b, d], iyr.at[yy, z], to_z(along_z(beside[b])))
 
     def iteration(step, carry):
         narrow = pt[...].astype(BF16)
-        for p, off in enumerate(pair_order):
-            q = lax.rem(zq + off, npair)
-            order = [*y_order, 0]
-            for n in range(0, len(order), 2):
-                parts = []
-                for d in order[n : n + 2]:
-                    base = lax.rem(y + d, ny) * rows + q * (2 * LANES)
-                    parts.append(nt(narrow, dv[pl.ds(pl.multiple_of(base, 2 * LANES), 2 * LANES), :]))
-                for d, part in zip(order[n : n + 2], parts):
-                    if d:
-                        s1[d - 1, p] = part.astype(BF16)
+        order = [*y_order, 0]
+        parts = [order[n : n + 2] for n in range(0, ny, 2)]
+
+        def beside_products(some):
+            made = products(narrow, some, beside)
+            for d, cut in made:
+                for b in range(2):
+                    s0[b, d] = cut[b].astype(BF16)
+            for d, _ in made:
+                for b in range(2):
+                    s0_copy(b, d).start()
+
+        def y_products(some, n, offsets):
+            sent = [o for o in offsets if o]
+            made = products(narrow, some, offsets)
+            for d, cut in made:
+                for m, part in enumerate(cut):
+                    if not d:
+                        acc1[n + m] = part
+                    elif offsets[m]:
+                        s1[d - 1, n + m] = part.astype(BF16)
                     else:
-                        acc1[p] = part
-                for d in order[n : n + 2]:
-                    if d:
-                        s1_copy(d, p).start()
-        for p, off in enumerate(pair_order):
-            tot = acc1[p]
-            for d in range(1, ny):
-                r1_copy(d, p).wait_recv()
-                tot = tot + r1[d - 1, p].astype(F32)
-            if off:
-                q = lax.rem(zq + off, npair)
-                for b in range(2):
-                    s2[p, b] = tot[:, b * LANES : (b + 1) * LANES].astype(BF16)
-                    s2_copy(p, b, 2 * q + b).start()
+                        acc0[d] = part
+            for d, _ in made:
+                if d and sent:
+                    s1_copy(d, n, len(sent)).start()
+
+        for some in parts:
+            y_products(some, *pairs[0])
+            beside_products(some)
+        for n, offsets in pairs[1:]:
+            for some in parts:
+                y_products(some, n, offsets)
+        last = len(distant)
+        for d in [*y_order, 0]:
+            for b in range(2):
+                s0_copy(b, d).wait_recv()
+            from_sides = r0[0, d].astype(F32) + r0[1, d].astype(F32)
+            if d:
+                s1[d - 1, last] = (acc0[d] + from_sides).astype(BF16)
+                s1_copy(d, last, 1).start()
             else:
-                own2[0] = tot[:, :LANES]
-                own2[1] = tot[:, LANES:]
-                s2[p, 0] = own2[1 - zb].astype(BF16)
-                s2_copy(p, 0, mate).start()
-        mine = own2[zb]
-        for d in range(1, nz):
-            zz = lax.rem(z + d, nz)
-            copy(s2.at[0, 0], r2.at[zz], s2s.at[0, 0], s2r.at[zz], to_z(zz)).wait_recv()
+                acc1[last] += from_sides
+        for n, offsets in pairs:
+            sent = [o for o in offsets if o]
+            if sent:
+                for d in range(1, ny):
+                    s1_copy(d, n, len(sent), True).wait_recv()
+            for m, o in enumerate(sent):
+                tot = acc1[n + m]
+                for d in range(1, ny):
+                    tot = tot + r1[d - 1, n + m].astype(F32)
+                s2[n + m] = tot.astype(BF16)
+            for m, o in enumerate(sent):
+                s2_copy(n + m, o).start()
+        mine = acc1[last]
+        for d in range(1, ny):
+            s1_copy(d, last, 1, True).wait_recv()
+            mine = mine + r1[d - 1, last].astype(F32)
+        for d in arriving[::-1]:
+            zz = along_z(d)
+            copy(s2.at[0], r2.at[zz], s2s.at[0], s2r.at[zz], to_z(zz)).wait_recv()
             mine = mine + r2[zz].astype(F32)
 
         img[y, z] = mine.astype(BF16)
-        for d in z_order:
-            zz = lax.rem(z + d, nz)
-            copy(img.at[y, z], img.at[y, z], izs.at[d], izr.at[z], to_z(zz)).start()
         for d in y_order:
             iy_copy(d, z, 0).start()
+        for d in [*distant, *beside]:
+            copy(img.at[y, z], img.at[y, z], izs.at[d], izr.at[z], to_z(along_z(d))).start()
 
         lanes = pl.ds(pl.multiple_of(j * LANES, LANES), LANES)
         p_own, r_own = pt[:, lanes], rt[:, lanes]
@@ -314,32 +377,45 @@
             copy(gxs.at[jj], gxr.at[j], gxss.at[d], gxsr.at[j], to_j(jj)).start()
         gxr[j] = gxs[j]
 
+        def arrived(d):
+            zz = along_z(d)
+            copy(img.at[y, zz], img.at[y, zz], izs.at[d], izr.at[zz], to_z(zz)).wait_recv()
+
         def forward(d):
-            zz = lax.rem(z + d, nz)
-            copy(img.at[y, zz], img.at[y, zz], izs.at[d], izr.at[zz], to_z(zz)).wait_recv()
+            arrived(d)
             for e in y_order:
-                iy_copy(e, zz, d).start()
+                iy_copy(e, along_z(d), d).start()
+
+        def y_arrived(d, zz):
+            yy = along_y(d)
+            copy(img.at[yy, zz], img.at[yy, zz], iys.at[d, 0], iyr.at[yy, zz], to_y(yy)).wait_recv()
 
         def project(yy):
             flat = jnp.concatenate([img[yy, zz] for zz in range(nz)], 1)
             return nn(flat, dv[pl.ds(pl.multiple_of(yy * rows, rows), rows), :])
 
-        for d in z_order[:4]:
+        for d in y_order[::-1]:
+            y_arrived(d, z)
+            for b in range(2):
+                if_copy(b, d).start()
+        for d in arriving[:2]:
+            forward(d)
+        for d in arriving[2:]:
             forward(d)
         wait_all(gxr, j, nxc, to_j, gxss, gxsr)
         gyr[y] = total(gxr, nxc)
         start_all(gyr, y, ny, to_y, gyss, gysr)
-        for d in z_order[4:]:
-            forward(d)
+        for d in beside:
+            arrived(d)
         qacc[...] = project(y)
-        wait_all(gyr, y, ny, to_y, gyss, gysr)
-        gzr[z] = total(gyr, ny)
-        start_all(gzr, z, nz, to_z, gzss, gzsr)
         for d in [e for e in (1, 3, 2) if e < ny]:
-            yy = lax.rem(y + d, ny)
-            for zz in range(nz):
-                copy(img.at[yy, zz], img.at[yy, zz], iys.at[d, 0], iyr.at[yy, zz], to_y(yy)).wait_recv()
-            qacc[...] += project(yy)
+            if d == y_order[0]:
+                wait_all(gyr, y, ny, to_y, gyss, gysr)
+                gzr[z] = total(gyr, ny)
+                start_all(gzr, z, nz, to_z, gzss, gzsr)
+            for o in range(1, nz):
+                y_arrived(d, along_z(o))
+            qacc[...] += project(along_y(d))
 
         for h in range(nc):
             qds[h] = qacc[:, h * half : (h + 1) * half]
@@ -356,9 +432,10 @@
             wait_all(gall, j, nxc, to_j, gass, gasr)
             gc = gall[...].reshape(k, 2 * k)
             inv = inverse(gc[:, :k])
-            ginv[...] = inv
             back[...] = nn_fine(gc[:, k:], inv)
-            xt[...] += nn_fine(back[...], pt[...])
+            old = tall(pt[...])
+            xt[...] += nn(wide(back[...]), old)
+            gp[...] = tall(nn(wide(inv), old))
 
         @pl.when(step + 1 == iters)
         def _():
@@ -390,24 +467,33 @@
             rt[...] -= nn_fine(back[...], qt[...])
             plane_finish()
             image = gathered()
-            small = block(nx - 1) + block(nx * nc - 1)
-            proj = yt[...] - nn_fine(back[...], image)
+            small = block(nx - 1).astype(F32) + block(nx * nc - 1).astype(F32)
+            weighted = image.astype(F32) * shrink[...]
+            inner = nt(jnp.concatenate([*halves(yt[...] * shrink[...]), *halves(weighted)], 0), image)
+            proj = yt[...] - rows_fine(back[...], nn, image)
             yt[...] = proj
-            scaled = proj * shrink[...]
-            cross = small[:, :k] - nn_fine(back[...], small[:, k:]) + nt_fine(scaled, image)
-            coef = nn_fine(cross, ginv[...])
-            pt[...] = rt[...] + spread(scaled) - nn_fine(coef, pt[...])
-
-        for p, off in enumerate(pair_order):
+            grown = small[:, k:] + inner[2 * k : 3 * k] + inner[3 * k :]
+            cross = small[:, :k] + inner[:k] + inner[k : 2 * k] - nn_fine(back[...], grown)
+            pt[...] = rt[...] + spread(proj * shrink[...]) - nn(wide(cross), gp[...])
+
+        for d in range(ny):
+            for b in range(2):
+                s0_copy(b, d).wait_send()
+        for n, offsets in pairs:
+            sent = [o for o in offsets if o]
             for d in range(1, ny):
-                s1_copy(d, p).wait_send()
-            for b in range(2 if off else 1):
-                s2_copy(p, b, mate).wait_send()
+                if sent:
+                    s1_copy(d, n, len(sent)).wait_send()
+            for m, o in enumerate(sent):
+                s2_copy(n + m, o).wait_send()
+        for d in range(1, ny):
+            s1_copy(d, last, 1).wait_send()
+            for b in range(2):
+                if_copy(b, d).wait_send()
+            for slot in [0, *distant]:
+                iy_copy(d, z, slot).wait_send()
         for d in range(1, nz):
-            copy(img.at[y, z], img.at[y, z], izs.at[d], izr.at[z], to_z(mate)).wait_send()
-        for e in range(1, ny):
-            for d in range(nz):
-                iy_copy(e, z, d).wait_send()
+            copy(img.at[y, z], img.at[y, z], izs.at[d], izr.at[z], to_z(along_z(d))).wait_send()
         for d in range(1, nxc):
             jj = lax.rem(j + d, nxc)
             copy(gxs.at[jj], gxr.at[j], gxss.at[d], gxsr.at[j], to_j(jj)).wait_send()
@@ -428,11 +514,12 @@
 def shards(sizes, design, right_side, factor, nystrom_values):
     nx, nf, nc, ny = sizes
     nz = nf // ny
-    nxc, npair = nx * nc, nz // 2
+    nxc = nx * nc
     samples, feats = design.shape
     k = right_side.shape[1] * nc
     rank_half = factor.shape[1]
     vmem = pl.BlockSpec(memory_space=pltpu.VMEM)
+    anywhere = pl.BlockSpec(memory_space=pl.ANY)
     dma = pltpu.SemaphoreType.DMA
     piece = (k // nxc, 2 * k)
     half = feats // nc
@@ -444,14 +531,16 @@
         pltpu.VMEM((k, feats), F32),
         pltpu.VMEM((k, feats), F32),
         pltpu.VMEM((k, nc * rank_half), F32),
-        pltpu.VMEM((k, k), F32),
+        pltpu.VMEM((4 * k, feats), BF16),
         pltpu.VMEM((k, feats), F32),
-        pltpu.VMEM((ny - 1, npair, k, 2 * LANES), BF16),
-        pltpu.VMEM((ny - 1, npair, k, 2 * LANES), BF16),
-        pltpu.VMEM((npair, k, 2 * LANES), F32),
-        pltpu.VMEM((npair, 2, k, LANES), BF16),
+        pltpu.VMEM((2, ny, k, LANES), BF16),
+        pltpu.VMEM((2, ny, k, LANES), BF16),
+        pltpu.VMEM((ny - 1, nz - 2, k, LANES), BF16),
+        pltpu.VMEM((ny - 1, nz - 2, k, LANES), BF16),
+        pltpu.VMEM((ny, k, LANES), F32),
+        pltpu.VMEM((nz - 2, k, LANES), F32),
+        pltpu.VMEM((nz - 3, k, LANES), BF16),
         pltpu.VMEM((nz, k, LANES), BF16),
-        pltpu.VMEM((2, k, LANES), F32),
         pltpu.VMEM((ny, nz, k, LANES), BF16),
         pltpu.VMEM((k, feats), F32),
         pltpu.VMEM((nxc, *piece), F32),
@@ -469,9 +558,9 @@
         pltpu.VMEM((nxc, ny, k // ny, LANES), BF16),
         pltpu.VMEM((k, k), F32),
         pltpu.VMEM((1, nc * rank_half), F32),
-        dma((ny,)), dma((2,)), dma((2,)),
-        dma((ny - 1, npair)), dma((ny - 1, npair)), dma((npair, 2)), dma((nz,)),
-        dma((nz,)), dma((nz,)), dma((ny, nz)), dma((ny, nz)),
+        dma((ny + 2,)), dma((2,)), dma((2,)),
+        dma((2, ny)), dma((2, ny)), dma((ny - 1, nz)), dma((ny - 1, nz)), dma((nz,)), dma((nz,)),
+        dma((nz,)), dma((nz,)), dma((ny, nz)), dma((ny, nz)), dma((2, ny)),
         dma((nxc,)), dma((nxc,)), dma((ny,)), dma((ny,)), dma((nz,)), dma((nz,)), dma((nxc,)), dma((nxc,)),
         dma((2,)), dma((nx,)), dma((nx,)), dma((2,)),
         dma((ny,)), dma((ny,)), dma((nz,)), dma((nz,)), dma((nxc * ny,)), dma((nxc, ny)),
@@ -479,14 +568,14 @@
     out = pl.pallas_call(
         functools.partial(kernel, (nx, nc, nz, ny, ITERS)),
         out_shape=jax.ShapeDtypeStruct((2, k // nc, feats), F32),
-        in_specs=[pl.BlockSpec(memory_space=pl.ANY), vmem, vmem, vmem],
+        in_specs=[anywhere, anywhere, anywhere, vmem],
         out_specs=vmem,
         scratch_shapes=scratch,
         compiler_params=pltpu.CompilerParams(
             collective_id=0, has_side_effects=True, vmem_limit_bytes=56 * 2**20
         ),
         name="solve",
-    )(design, right_side.T, factor, nystrom_values[None, :])
+    )(design, right_side.T, factor, nystrom_values.reshape(-1, LANES))
     return out[0].T, out[1].T
 
 

time: 166 us -> 155 us (0.934)
  Pallas kernels: 163 us -> 153 us
    pallas_call x1, Pallas kernels: 163 us -> 153 us  [shards(): pl.pallas_call(functools.partial(kernel, (nx, nc, nz, ny, ITERS)), out_sh...]
where the time goes in v3:
time: 155 us
  Pallas kernels  153 us (99%)
  local copies, waits for them, and re-layouts  1.69 us (1%)
    pallas_call x1, Pallas kernels, shards(): pl.pallas_call(functools.partial(kernel, (nx, nc, nz, ny, ITERS)), out_sh...  153 us

profile of v3, /device:TPU:1, one launch (start us, length us, event | category | flops | bytes accessed | tf_op | source)
XLA Modules:
  0.0 155.0 jit_solution(1309054948424923580)
XLA Ops:
  0.6 152.7 %solve.1 = f32[2,32,1024]{2,1,0:T(8,128)} custom-call(bf16[4096,1024]{1,0:T(8,128)(2,1)} %d_hbm.1, f32[32,1024]{1,0:T(8,128)} %bitcast.10, bf16[1024,384]{1,0:T(8,128)(2,1)} %f_in.1, f32[6,128]{1,0:T(8,128)} %bitcast.11), custom_call_target="tpu_custom_call" | custom-call | tf_op jit(solution)/shard_map/solve/pallas_call | solution.py:568
  153.3 1.7 %slice_bitcast_fusion = (f32[1024,32]{0,1:T(8,128)}, f32[1024,32]{0,1:T(8,128)}) fusion(f32[2,32,1024]{2,1,0:T(8,128)} %solve.1), kind=kLoop, calls=%fused_computation | loop fusion | bytes 524288 | tf_op jit(solution)/shard_map/transpose | solution.py:579

commit v4 on v3

--- a/solution.py
+++ b/solution.py
@@ -87,12 +87,12 @@
     out,
     dv, rfull, fall, pt, rt, xt, yt, gp, qt,
     s0, r0, s1, r1, acc0, acc1, s2, r2, img, qacc,
-    gxs, gxr, gyr, gzr, gall,
+    gxs, gxr, gmr, gyr, gzr, gall,
     qds, qdr, qxr, qf,
     wys, wyr, wzr, wall, back, shrink,
     dsem, rsem, fsem,
     s0s, s0r, s1s, s1r, s2s, s2r, izs, izr, iys, iyr, ifs,
-    gxss, gxsr, gyss, gysr, gzss, gzsr, gass, gasr,
+    gxss, gxsr, gmss, gmsr, gyss, gysr, gzss, gzsr, gass, gasr,
     qdsem, qxss, qxsr, qfsem,
     wyss, wysr, wzss, wzsr, wxss, wxsr,
 ):
@@ -158,12 +158,17 @@
             t = t + ref[i].astype(F32)
         return t
 
+    def f_lanes(cc):
+        return pl.ds(pl.multiple_of(cc * rank_half, LANES), rank_half)
+
+    own_half = pl.ds(pl.multiple_of(c * half, LANES), half)
+
     loads = [
         pltpu.make_async_copy(d_hbm.at[pl.ds(i * rows, rows)], dv.at[pl.ds(i * rows, rows)], dsem.at[i])
         for i in range(ny)
     ]
     load_r = pltpu.make_async_copy(rt_in, rfull.at[c], dsem.at[ny])
-    load_f = pltpu.make_async_copy(f_in, fall.at[c], dsem.at[ny + 1])
+    load_f = pltpu.make_async_copy(f_in, fall.at[:, f_lanes(c)], dsem.at[ny + 1])
     load_r.start()
     load_f.start()
     for load in loads:
@@ -180,21 +185,39 @@
     send_r = copy(rfull.at[c], rfull.at[c], rsem.at[0], rsem.at[1], to_core())
     send_r.start()
     load_f.wait()
-    send_f = copy(fall.at[c], fall.at[c], fsem.at[0], fsem.at[1], to_core())
+    send_f = copy(fall.at[:, f_lanes(c)], fall.at[:, f_lanes(c)], fsem.at[0], fsem.at[1], to_core())
     send_f.start()
 
     quarter = k // ny
 
-    def plane_sum(value):
-        wys[...] = value.reshape(wys.shape)
-        for d in range(1, ny):
-            yy = lax.rem(y + d, ny)
-            copy(wys.at[yy], wyr.at[y], wyss.at[d], wysr.at[y], to_y(yy)).start()
-        wyr[y] = wys[y]
-
-    def plane_exchange():
-        wait_all(wyr, y, ny, to_y, wyss, wysr)
-        wzr[z] = total(wyr, ny)
+    over_y = [(d, 0) for d in range(1, ny)]
+    over_yc = [(d, 0) for d in range(1, ny)] + [(d, 1) for d in range(ny)]
+
+    def sum_copy(n, offset, received=False):
+        yy, cc = lax.rem(y + offset[0], ny), lax.rem(c + offset[1], nc)
+        slot = cc * ny + yy if received else c * ny + y
+        return copy(wys.at[cc, yy], wyr.at[slot], wyss.at[n], wysr.at[slot], to_near(yy, x, cc))
+
+    def plane_sum(value, offsets):
+        if offsets is over_y:
+            wys[c] = value.reshape(wys.shape[1:])
+        else:
+            for cc in range(nc):
+                wys[cc] = value[:, cc * LANES : (cc + 1) * LANES].reshape(wys.shape[1:])
+        for n, offset in enumerate(offsets):
+            sum_copy(n, offset).start()
+        wyr[c * ny + y] = wys[c, y]
+
+    def plane_exchange(offsets):
+        for n, offset in enumerate(offsets):
+            sum_copy(n, offset, True).wait_recv()
+        if offsets is over_y:
+            t = wyr[c * ny]
+            for i in range(1, ny):
+                t = t + wyr[c * ny + i]
+            wzr[z] = t
+        else:
+            wzr[z] = total(wyr, nc * ny)
         start_all(wzr, z, nz, to_z, wzss, wzsr)
 
     def near_copy(n, offset, source):
@@ -203,7 +226,7 @@
             return copy(wall.at[cc * nx + xx, yy], wall.at[cc * nx + xx, yy], wxss.at[n], wxsr.at[cc * nx + xx, yy], to_near(yy, xx, cc))
         return copy(wall.at[j, y], wall.at[j, y], wxss.at[n], wxsr.at[j, y], to_near(yy, xx, cc))
 
-    def plane_finish():
+    def plane_finish(offsets):
         wait_all(wzr, z, nz, to_z, wzss, wzsr)
         whole = total(wzr, nz)
         upper, lower = halves(whole)
@@ -212,9 +235,8 @@
             near_copy(n, offset, False).start()
         for n, offset in enumerate(near):
             near_copy(n, offset, True).wait_recv()
-        for d in range(1, ny):
-            yy = lax.rem(y + d, ny)
-            copy(wys.at[yy], wyr.at[y], wyss.at[d], wysr.at[y], to_y(yy)).wait_send()
+        for n, offset in enumerate(offsets):
+            sum_copy(n, offset).wait_send()
         sent_all(wzr, z, nz, to_z, wzss, wzsr)
         for n, offset in enumerate(near):
             near_copy(n, offset, False).wait_send()
@@ -222,15 +244,11 @@
     def block(jj):
         return wall[jj].reshape(k, LANES)
 
-    def gathered():
-        return jnp.concatenate([block(cc * nx + b) for cc in range(nc) for b in range(nblk)], 1)
-
-    def own_block(value):
-        return rows_fine(value, nn, fall[c, :, pl.ds(pl.multiple_of(x * LANES, LANES), LANES)])
+    def gathered(slots):
+        return jnp.concatenate([block(jj) for jj in slots], 1)
 
     def spread(scaled):
-        out = rows_fine(scaled[:, :rank_half], nt, fall[0])
-        return out + rows_fine(scaled[:, rank_half:], nt, fall[1])
+        return rows_fine(scaled, nt, fall[...])
 
     least = jnp.min(jnp.min(values[...], axis=1, keepdims=True), axis=0, keepdims=True)
     table = (1.0 + least) / (1.0 + values[...]) - 1.0
@@ -242,18 +260,19 @@
 
     @pl.when(x < nblk)
     def _():
-        plane_sum(own_block(rt[...]))
+        lanes = pl.ds(pl.multiple_of(c * rank_half + x * LANES, LANES), LANES)
+        plane_sum(rows_fine(rt[...], nn, fall[:, lanes]), over_y)
 
     @pl.when(x == nblk)
     def _():
-        plane_sum(jnp.zeros((k, LANES), F32))
-
-    plane_exchange()
-    plane_finish()
-    copy(fall.at[c], fall.at[other], fsem.at[0], fsem.at[1], to_core()).wait_recv()
+        plane_sum(jnp.zeros((k, LANES), F32), over_y)
+
+    plane_exchange(over_y)
+    plane_finish(over_y)
+    copy(fall.at[:, f_lanes(c)], fall.at[:, f_lanes(other)], fsem.at[0], fsem.at[1], to_core()).wait_recv()
     send_r.wait_send()
     send_f.wait_send()
-    yt[...] = gathered().astype(F32)
+    yt[...] = gathered([cc * nx + b for cc in range(nc) for b in range(nblk)]).astype(F32)
     pt[...] = rt[...] + spread(yt[...] * shrink[...])
     for load in loads:
         load.wait()
@@ -326,21 +345,13 @@
 
         for some in parts:
             y_products(some, *pairs[0])
+        for some in parts:
             beside_products(some)
         for n, offsets in pairs[1:]:
             for some in parts:
                 y_products(some, n, offsets)
-        last = len(distant)
-        for d in [*y_order, 0]:
-            for b in range(2):
-                s0_copy(b, d).wait_recv()
-            from_sides = r0[0, d].astype(F32) + r0[1, d].astype(F32)
-            if d:
-                s1[d - 1, last] = (acc0[d] + from_sides).astype(BF16)
-                s1_copy(d, last, 1).start()
-            else:
-                acc1[last] += from_sides
-        for n, offsets in pairs:
+
+        def y_summed(n, offsets):
             sent = [o for o in offsets if o]
             if sent:
                 for d in range(1, ny):
@@ -352,6 +363,21 @@
                 s2[n + m] = tot.astype(BF16)
             for m, o in enumerate(sent):
                 s2_copy(n + m, o).start()
+
+        if len(pairs) > 1:
+            y_summed(*pairs[0])
+        last = len(distant)
+        for d in [*y_order, 0]:
+            for b in range(2):
+                s0_copy(b, d).wait_recv()
+            from_sides = r0[0, d].astype(F32) + r0[1, d].astype(F32)
+            if d:
+                s1[d - 1, last] = (acc0[d] + from_sides).astype(BF16)
+                s1_copy(d, last, 1).start()
+            else:
+                acc1[last] += from_sides
+        for n, offsets in pairs[1:] if len(pairs) > 1 else pairs:
+            y_summed(n, offsets)
         mine = acc1[last]
         for d in range(1, ny):
             s1_copy(d, last, 1, True).wait_recv()
@@ -372,10 +398,28 @@
         both = jnp.concatenate([mine, p_own], 1)
         gc = jnp.concatenate([nt_fine(both, both), nt_fine(r_own, p_own)], 1)
         gxs[...] = gc.reshape(gxs.shape)
-        for d in range(1, nxc):
+
+        def gx_copy(d):
             jj = lax.rem(j + d, nxc)
-            copy(gxs.at[jj], gxr.at[j], gxss.at[d], gxsr.at[j], to_j(jj)).start()
-        gxr[j] = gxs[j]
+            return copy(gxs.at[jj], gxr.at[j], gxss.at[d], gxsr.at[j], to_j(jj))
+
+        def gm_copy(n, offset, received=False):
+            yy, xx, cc = moved(offset)
+            jj = cc * nx + xx
+            slot = jj * ny + yy if received else j * ny + y
+            return copy(gxs.at[jj], gmr.at[slot], gmss.at[n], gmsr.at[slot], to_near(yy, xx, cc))
+
+        @pl.when(step + 1 < iters)
+        def _():
+            for d in range(1, nxc):
+                gx_copy(d).start()
+            gxr[j] = gxs[j]
+
+        @pl.when(step + 1 == iters)
+        def _():
+            for n, offset in enumerate(near):
+                gm_copy(n, offset).start()
+            gmr[j * ny + y] = gxs[j]
 
         def arrived(d):
             zz = along_z(d)
@@ -402,17 +446,30 @@
             forward(d)
         for d in arriving[2:]:
             forward(d)
-        wait_all(gxr, j, nxc, to_j, gxss, gxsr)
-        gyr[y] = total(gxr, nxc)
-        start_all(gyr, y, ny, to_y, gyss, gysr)
+        @pl.when(step + 1 < iters)
+        def _():
+            wait_all(gxr, j, nxc, to_j, gxss, gxsr)
+            gyr[y] = total(gxr, nxc)
+            start_all(gyr, y, ny, to_y, gyss, gysr)
+
+        @pl.when(step + 1 == iters)
+        def _():
+            for n, offset in enumerate(near):
+                gm_copy(n, offset, True).wait_recv()
+            gzr[z] = total(gmr, nxc * ny)
+            start_all(gzr, z, nz, to_z, gzss, gzsr)
+
         for d in beside:
             arrived(d)
         qacc[...] = project(y)
         for d in [e for e in (1, 3, 2) if e < ny]:
             if d == y_order[0]:
-                wait_all(gyr, y, ny, to_y, gyss, gysr)
-                gzr[z] = total(gyr, ny)
-                start_all(gzr, z, nz, to_z, gzss, gzsr)
+                @pl.when(step + 1 < iters)
+                def _():
+                    wait_all(gyr, y, ny, to_y, gyss, gysr)
+                    gzr[z] = total(gyr, ny)
+                    start_all(gzr, z, nz, to_z, gzss, gzsr)
+
             for o in range(1, nz):
                 y_arrived(d, along_z(o))
             qacc[...] += project(along_y(d))
@@ -421,21 +478,41 @@
             qds[h] = qacc[:, h * half : (h + 1) * half]
         qd = copy(qds.at[other], qdr, qdsem.at[0], qdsem.at[1], to_core())
         qd.start()
-        qd.wait_recv()
-        qxr[x] = (qds[c] + qdr[...]).astype(BF16)
-        start_all(qxr, x, nx, to_x, qxss, qxsr)
-        wait_all(gzr, z, nz, to_z, gzss, gzsr)
-        gall[j] = total(gzr, nz)
-        start_all(gall, j, nxc, to_j, gass, gasr)
+        def sums_along_x():
+            qd.wait_recv()
+            qxr[x] = (qds[c] + qdr[...]).astype(BF16)
+            start_all(qxr, x, nx, to_x, qxss, qxsr)
+
+        def gram_to_all():
+            wait_all(gzr, z, nz, to_z, gzss, gzsr)
+            gall[j] = total(gzr, nz)
+            start_all(gall, j, nxc, to_j, gass, gasr)
+
+        @pl.when(step + 1 < iters)
+        def _():
+            sums_along_x()
+            gram_to_all()
+
+        @pl.when(step + 1 == iters)
+        def _():
+            gram_to_all()
+            sums_along_x()
 
         def step_coefficient():
             wait_all(gall, j, nxc, to_j, gass, gasr)
             gc = gall[...].reshape(k, 2 * k)
             inv = inverse(gc[:, :k])
             back[...] = nn_fine(gc[:, k:], inv)
+            return inv
+
+        def advance():
             old = tall(pt[...])
             xt[...] += nn(wide(back[...]), old)
-            gp[...] = tall(nn(wide(inv), old))
+            return old
+
+        def join_halves():
+            copy(qf.at[other], qf.at[other], qfsem.at[0], qfsem.at[1], to_core()).wait_recv()
+            qt[...] = jnp.concatenate([qf[h] for h in range(nc)], 1) + pt[...]
 
         @pl.when(step + 1 == iters)
         def _():
@@ -445,28 +522,34 @@
         qf[c] = total(qxr, nx)
         qfc = copy(qf.at[c], qf.at[c], qfsem.at[0], qfsem.at[1], to_core())
         qfc.start()
-        copy(qf.at[other], qf.at[other], qfsem.at[0], qfsem.at[1], to_core()).wait_recv()
-        qt[...] = jnp.concatenate([qf[h] for h in range(nc)], 1) + pt[...]
 
         @pl.when(step + 1 == iters)
         def _():
+            advance()
+            join_halves()
             rt[...] -= nn_fine(back[...], qt[...])
 
         @pl.when(step + 1 < iters)
         def _():
+            q_half = qf[c] + pt[:, own_half]
+
             @pl.when(x < nblk)
             def _():
-                plane_sum(own_block(qt[...]))
+                lanes = pl.ds(pl.multiple_of(x * (nc * LANES), nc * LANES), nc * LANES)
+                plane_sum(rows_fine(q_half, nn, fall[own_half, lanes]), over_yc)
 
             @pl.when(x == nblk)
             def _():
-                plane_sum(jnp.concatenate([nt_fine(rt[...], qt[...]), nt_fine(qt[...], qt[...])], 1))
-
-            plane_exchange()
-            step_coefficient()
+                both = jnp.concatenate([nt_fine(rt[:, own_half], q_half), nt_fine(q_half, q_half)], 1)
+                plane_sum(jnp.concatenate([both] * nc, 1), over_yc)
+
+            join_halves()
+            plane_exchange(over_yc)
+            inv = step_coefficient()
+            gp[...] = tall(nn(wide(inv), advance()))
             rt[...] -= nn_fine(back[...], qt[...])
-            plane_finish()
-            image = gathered()
+            plane_finish(over_yc)
+            image = gathered([cc * nx + b for b in range(nblk) for cc in range(nc)])
             small = block(nx - 1).astype(F32) + block(nx * nc - 1).astype(F32)
             weighted = image.astype(F32) * shrink[...]
             inner = nt(jnp.concatenate([*halves(yt[...] * shrink[...]), *halves(weighted)], 0), image)
@@ -494,10 +577,17 @@
                 iy_copy(d, z, slot).wait_send()
         for d in range(1, nz):
             copy(img.at[y, z], img.at[y, z], izs.at[d], izr.at[z], to_z(along_z(d))).wait_send()
-        for d in range(1, nxc):
-            jj = lax.rem(j + d, nxc)
-            copy(gxs.at[jj], gxr.at[j], gxss.at[d], gxsr.at[j], to_j(jj)).wait_send()
-        sent_all(gyr, y, ny, to_y, gyss, gysr)
+        @pl.when(step + 1 < iters)
+        def _():
+            for d in range(1, nxc):
+                gx_copy(d).wait_send()
+            sent_all(gyr, y, ny, to_y, gyss, gysr)
+
+        @pl.when(step + 1 == iters)
+        def _():
+            for n, offset in enumerate(near):
+                gm_copy(n, offset).wait_send()
+
         sent_all(gzr, z, nz, to_z, gzss, gzsr)
         sent_all(gall, j, nxc, to_j, gass, gasr)
         qd.wait_send()
@@ -526,7 +616,7 @@
     scratch = [
         pltpu.VMEM((samples, feats), BF16),
         pltpu.VMEM((nc, k // nc, feats), F32),
-        pltpu.VMEM((nc, feats, rank_half), BF16),
+        pltpu.VMEM((feats, nc * rank_half), BF16),
         pltpu.VMEM((k, feats), F32),
         pltpu.VMEM((k, feats), F32),
         pltpu.VMEM((k, feats), F32),
@@ -545,6 +635,7 @@
         pltpu.VMEM((k, feats), F32),
         pltpu.VMEM((nxc, *piece), F32),
         pltpu.VMEM((nxc, *piece), F32),
+        pltpu.VMEM((nxc * ny, *piece), F32),
         pltpu.VMEM((ny, *piece), F32),
         pltpu.VMEM((nz, *piece), F32),
         pltpu.VMEM((nxc, *piece), F32),
@@ -552,8 +643,8 @@
         pltpu.VMEM((k, half), F32),
         pltpu.VMEM((nx, k, half), BF16),
         pltpu.VMEM((nc, k, half), F32),
-        pltpu.VMEM((ny, k // ny, LANES), F32),
-        pltpu.VMEM((ny, k // ny, LANES), F32),
+        pltpu.VMEM((nc, ny, k // ny, LANES), F32),
+        pltpu.VMEM((nc * ny, k // ny, LANES), F32),
         pltpu.VMEM((nz, k // ny, LANES), F32),
         pltpu.VMEM((nxc, ny, k // ny, LANES), BF16),
         pltpu.VMEM((k, k), F32),
@@ -561,9 +652,10 @@
         dma((ny + 2,)), dma((2,)), dma((2,)),
         dma((2, ny)), dma((2, ny)), dma((ny - 1, nz)), dma((ny - 1, nz)), dma((nz,)), dma((nz,)),
         dma((nz,)), dma((nz,)), dma((ny, nz)), dma((ny, nz)), dma((2, ny)),
-        dma((nxc,)), dma((nxc,)), dma((ny,)), dma((ny,)), dma((nz,)), dma((nz,)), dma((nxc,)), dma((nxc,)),
+        dma((nxc,)), dma((nxc,)), dma((nxc * ny,)), dma((nxc * ny,)), dma((ny,)), dma((ny,)),
+        dma((nz,)), dma((nz,)), dma((nxc,)), dma((nxc,)),
         dma((2,)), dma((nx,)), dma((nx,)), dma((2,)),
-        dma((ny,)), dma((ny,)), dma((nz,)), dma((nz,)), dma((nxc * ny,)), dma((nxc, ny)),
+        dma((nc * ny,)), dma((nc * ny,)), dma((nz,)), dma((nz,)), dma((nxc * ny,)), dma((nxc, ny)),
     ]
     out = pl.pallas_call(
         functools.partial(kernel, (nx, nc, nz, ny, ITERS)),

time: 155 us -> 148 us (0.955)
  Pallas kernels: 153 us -> 146 us
    pallas_call x1, Pallas kernels: 153 us -> 146 us  [shards(): pl.pallas_call(functools.partial(kernel, (nx, nc, nz, ny, ITERS)), out_sh...]
where the time goes in v4:
time: 148 us
  Pallas kernels  146 us (99%)
  local copies, waits for them, and re-layouts  1.69 us (1%)
    pallas_call x1, Pallas kernels, shards(): pl.pallas_call(functools.partial(kernel, (nx, nc, nz, ny, ITERS)), out_sh...  146 us

profile of v4, /device:TPU:1, one launch (start us, length us, event | category | flops | bytes accessed | tf_op | source)
XLA Modules:
  0.0 148.2 jit_solution(1212804661116759475)
XLA Ops:
  0.6 145.8 %solve.1 = f32[2,32,1024]{2,1,0:T(8,128)} custom-call(bf16[4096,1024]{1,0:T(8,128)(2,1)} %d_hbm.1, f32[32,1024]{1,0:T(8,128)} %bitcast.10, bf16[1024,384]{1,0:T(8,128)(2,1)} %f_in.1, f32[6,128]{1,0:T(8,128)} %bitcast.11), custom_call_target="tpu_custom_call" | custom-call | tf_op jit(solution)/shard_map/solve/pallas_call | solution.py:660
  146.5 1.7 %slice_bitcast_fusion = (f32[1024,32]{0,1:T(8,128)}, f32[1024,32]{0,1:T(8,128)}) fusion(f32[2,32,1024]{2,1,0:T(8,128)} %solve.1), kind=kLoop, calls=%fused_computation | loop fusion | bytes 524288 | tf_op jit(solution)/shard_map/transpose | solution.py:671

commit v5 on v4

--- a/solution.py
+++ b/solution.py
@@ -137,8 +137,11 @@
             src_ref=src, dst_ref=dst, send_sem=ss, recv_sem=rs, device_id=dev, device_id_type=MESH
         )
 
+    def far_first(n, ring):
+        return sorted(range(1, n), key=lambda d: -min(d % ring, ring - d % ring))
+
     def start_all(ref, me, n, to, ss, rs):
-        for d in range(1, n):
+        for d in far_first(n, nx if to is to_j else n):
             other_one = lax.rem(me + d, n)
             copy(ref.at[me], ref.at[me], ss.at[d], rs.at[me], to(other_one)).start()
 
@@ -190,8 +193,8 @@
 
     quarter = k // ny
 
-    over_y = [(d, 0) for d in range(1, ny)]
-    over_yc = [(d, 0) for d in range(1, ny)] + [(d, 1) for d in range(ny)]
+    over_y = [(d, 0) for d in far_first(ny, ny)]
+    over_yc = [(d, e) for d in [*far_first(ny, ny), 0] for e in range(nc) if d or e]
 
     def sum_copy(n, offset, received=False):
         yy, cc = lax.rem(y + offset[0], ny), lax.rem(c + offset[1], nc)
@@ -411,7 +414,7 @@
 
         @pl.when(step + 1 < iters)
         def _():
-            for d in range(1, nxc):
+            for d in far_first(nxc, nx):
                 gx_copy(d).start()
             gxr[j] = gxs[j]
 

time: 148 us -> 148 us (level)
  no operation moved by 1% of the time
where the time goes in v5:
time: 148 us
  Pallas kernels  145 us (98%)
  local copies, waits for them, and re-layouts  1.69 us (1%)
    pallas_call x1, Pallas kernels, shards(): pl.pallas_call(functools.partial(kernel, (nx, nc, nz, ny, ITERS)), out_sh...  145 us

profile of v5, /device:TPU:1, one launch (start us, length us, event | category | flops | bytes accessed | tf_op | source)
XLA Modules:
  0.0 147.6 jit_solution(7827558798996626870)
XLA Ops:
  0.6 145.3 %solve.1 = f32[2,32,1024]{2,1,0:T(8,128)} custom-call(bf16[4096,1024]{1,0:T(8,128)(2,1)} %d_hbm.1, f32[32,1024]{1,0:T(8,128)} %bitcast.10, bf16[1024,384]{1,0:T(8,128)(2,1)} %f_in.1, f32[6,128]{1,0:T(8,128)} %bitcast.11), custom_call_target="tpu_custom_call" | custom-call | tf_op jit(solution)/shard_map/solve/pallas_call | solution.py:663
  145.9 1.7 %slice_bitcast_fusion = (f32[1024,32]{0,1:T(8,128)}, f32[1024,32]{0,1:T(8,128)}) fusion(f32[2,32,1024]{2,1,0:T(8,128)} %solve.1), kind=kLoop, calls=%fused_computation | loop fusion | bytes 524288 | tf_op jit(solution)/shard_map/transpose | solution.py:674
